TPU v7x, 512 devices: a whole 4x8x8 slice. The times are simulated.
512 devices in a mesh: wn: 16 (over y, core), sp: 32 (over x, z).
Axes of the slice: x: 4, y: 8, z: 8, core: 2. Of those that a mesh axis runs over, the one named last changes fastest.
Arguments:
- random_slabs: float32 [8, 3, 2048, 4096], P(None, None, 'wn', 'sp'), may hold values from -6 to 6
- stress: float32 [6, 2048], P(None, 'wn'), may hold values from -0.8 to 2, as said below
- profile: float32 [2048], P('wn'), may hold values from 0.2 to 1.2
Outputs:
- inflow: float32 [8, 3, 2048, 4096], P(None, None, 'wn', 'sp')
Inputs may be any that keep to these rules, and one draw needn't show every extreme that they name: R11, R22 and R33 are positive, and each off-diagonal stress is at most 0.4 times the square root of the product of its two diagonal stresses in magnitude.
All inputs are finite; a program needn't handle non-finite values.
Results may differ from a plain program's by a relative error of at most 0.0003.
Values sent between devices are 32-bit elements; how exact they have to be, the bound alone decides.
No kernel may reach another device: no remote copies, remote signals or barrier semaphores. Data moves between devices by JAX's collectives and lax.ppermute only.
A program may use at most 128 MiB of HBM per device.

v0:
```python
import jax
import jax.numpy as jnp
from jax import lax
from jax.sharding import PartitionSpec as P

H = 64


epsilon = 1e-06


def with_halo(block, sides, width, periodic):
    for axis, dim in sides:
        count = lax.axis_size(axis)
        forward = [(i, i + 1) for i in range(count - 1)]
        if periodic:
            forward.append((count - 1, 0))
        backward = [(target, source) for source, target in forward]
        low = lax.ppermute(
            lax.slice_in_dim(block, block.shape[dim] - width, None, axis=dim), axis, forward
        )
        high = lax.ppermute(lax.slice_in_dim(block, 0, width, axis=dim), axis, backward)
        block = jnp.concatenate([low, block, high], axis=dim)
    return block


def from_everyone(x, axis):
    peers = lax.axis_size(axis)
    return lax.all_to_all(jnp.broadcast_to(x[None], (peers, *x.shape)), axis, 0, 0, tiled=True)


def taken_together(x, axis):
    return from_everyone(x, axis).sum(axis=0)


def together(arrays, axis):
    ends = [0]
    for a in arrays:
        ends.append(ends[-1] + a.size)
    so_far = taken_together(jnp.concatenate([a.ravel() for a in arrays]), axis)
    return tuple((so_far[b:e].reshape(a.shape) for a, b, e in zip(arrays, ends, ends[1:])))


def band_matrix(reach):
    width = 2 * reach
    offset = jnp.arange(-reach, reach + 1).astype(jnp.float32)
    scale_len = reach / 2.0
    norming = jnp.sqrt(jnp.sum(jnp.exp(-jnp.pi * offset * offset / (scale_len * scale_len))))
    source = jnp.arange(2 * width)[:, None]
    target = jnp.arange(width)[None, :]
    lag = (source - target - reach).astype(jnp.float32)
    values = jnp.exp(-jnp.pi * lag * lag / (2.0 * scale_len * scale_len)) / norming
    return jnp.where(jnp.abs(lag) <= reach, values, 0.0)


def filter_last(padded, reach):
    width = 2 * reach
    band = band_matrix(reach)
    lead = padded.shape[:-1]
    blocks = padded.reshape(lead + (padded.shape[-1] // width, width))
    upper = jnp.matmul(blocks[..., :-1, :], band[:width], precision=lax.Precision.HIGHEST)
    lower = jnp.matmul(blocks[..., 1:, :], band[width:], precision=lax.Precision.HIGHEST)
    return (upper + lower).reshape(lead + (padded.shape[-1] - width,))


def filter_rows(padded, reach):
    width = 2 * reach
    band = band_matrix(reach)
    steps_n, comps, length, cols = padded.shape
    blocks = padded.reshape(steps_n, comps, length // width, width, cols)
    upper = jnp.einsum(
        "scbjz,ji->scbiz", blocks[:, :, :-1], band[:width], precision=lax.Precision.HIGHEST
    )
    lower = jnp.einsum(
        "scbjz,ji->scbiz", blocks[:, :, 1:], band[width:], precision=lax.Precision.HIGHEST
    )
    return (upper + lower).reshape(steps_n, comps, length - width, cols)


def lund(scaled, stress, profile):
    chol_xx = jnp.sqrt(stress[0])
    chol_yx = stress[3] / chol_xx
    chol_yy = jnp.sqrt(stress[1] - chol_yx * chol_yx)
    chol_zx = stress[4] / chol_xx
    chol_zy = (stress[5] - chol_yx * chol_zx) / chol_yy
    chol_zz = jnp.sqrt(stress[2] - chol_zx * chol_zx - chol_zy * chol_zy)
    first = profile[:, None] + chol_xx[:, None] * scaled[:, 0]
    second = chol_yx[:, None] * scaled[:, 0] + chol_yy[:, None] * scaled[:, 1]
    third = (
        chol_zx[:, None] * scaled[:, 0]
        + chol_zy[:, None] * scaled[:, 1]
        + chol_zz[:, None] * scaled[:, 2]
    )
    return jnp.stack([first, second, third], axis=1)


def body(random_slabs, stress, profile):
    padded = with_halo(random_slabs, (("wn", 2),), H, False)
    normal_pass = filter_rows(padded, H)
    span_total = lax.axis_size("sp") * normal_pass.shape[3]
    wrapped = with_halo(normal_pass, (("sp", 3),), H, True)
    filtered = filter_last(wrapped, H)
    sum_first, sum_second = together(
        (jnp.sum(filtered, axis=-1), jnp.sum(filtered * filtered, axis=-1)), "sp"
    )
    row_mean = sum_first / span_total
    centred = filtered - row_mean[..., None]
    row_var = sum_second / span_total - row_mean * row_mean
    scaled = centred / jnp.sqrt(row_var[..., None] + epsilon)
    return lund(scaled, stress, profile)


def solution(mesh):
    return jax.shard_map(
        body,
        mesh=mesh,
        in_specs=(P(None, None, "wn", "sp"), P(None, "wn"), P("wn")),
        out_specs=P(None, None, "wn", "sp"),
        check_vma=False,
    )
```

profile of v0, /device:TPU:48, one launch (start us, length us, event | category | flops | bytes accessed | tf_op | source)
XLA Modules:
  0.0 95.7 jit_solution(4993913002920604992)
XLA Ops:
  0.0 2.8 %fusion.21 = (f32[8,3,64,128]{3,2,1,0:T(8,128)}, f32[8,3,64,128]{3,2,1,0:T(8,128)}) fusion(f32[8,3,128,128]{3,2,1,0:T(8,128)} %param.3), kind=kLoop, calls=%fused_computation.51 | loop fusion | bytes 3145728 | tf_op jit(solution)/shard_map/slice | solution.py:20
  2.8 1.9 %collective-permute-start = (f32[8,3,64,128]{3,2,1,0:T(8,128)}, f32[8,3,64,128]{3,2,1,0:T(8,128)S(1)}, u32[]{:S(2)}, u32[]{:S(2)}) collective-permute-start(f32[8,3,64,128]{3,2,1,0:T(8,128)} %get-tuple-element.16), channel_id=1, source_target_pairs={{0,32},{32,64},{64,96},{96,128},{128,160},{160,192},{192,224},{224... | collective-permute-start | bytes 2359304 | tf_op jit(solution)/shard_map/ppermute | solution.py:19
  4.7 3.6 %collective-permute-start.1 = (f32[8,3,64,128]{3,2,1,0:T(8,128)}, f32[8,3,64,128]{3,2,1,0:T(8,128)S(1)}, u32[]{:S(2)}, u32[]{:S(2)}) collective-permute-start(f32[8,3,64,128]{3,2,1,0:T(8,128)} %get-tuple-element.17), channel_id=1, source_target_pairs={{32,0},{64,32},{96,64},{128,96},{160,128},{192,160},{224,192},{256... | collective-permute-start | bytes 2359304 | tf_op jit(solution)/shard_map/ppermute | solution.py:22
  8.4 0.7 fusion.12
  9.8 6.5 %collective-permute-done = f32[8,3,64,128]{3,2,1,0:T(8,128)S(1)} collective-permute-done((f32[8,3,64,128]{3,2,1,0:T(8,128)}, f32[8,3,64,128]{3,2,1,0:T(8,128)S(1)}, u32[]{:S(2)}, u32[]{:S(2)}) %collective-permute-start) | collective-permute-done | bytes 786464 | tf_op jit(solution)/shard_map/ppermute | solution.py:19
  16.3 1.9 %collective-permute-done.1 = f32[8,3,64,128]{3,2,1,0:T(8,128)S(1)} collective-permute-done((f32[8,3,64,128]{3,2,1,0:T(8,128)}, f32[8,3,64,128]{3,2,1,0:T(8,128)S(1)}, u32[]{:S(2)}, u32[]{:S(2)}) %collective-permute-start.1) | collective-permute-done | bytes 786464 | tf_op jit(solution)/shard_map/ppermute | solution.py:22
  18.2 0.2 pad_maximum_fusion
  18.4 2.7 %fusion.2 = f32[128,8,3,128]{0,3,2,1:T(8,128)S(1)} fusion(f32[8,3,2,128,128]{4,3,2,1,0:T(8,128)S(1)} %bitcast.90, f32[256,128]{1,0:T(8,128)S(1)} %fusion.9), kind=kOutput, calls=%fused_computation.7 | convolution fusion | flops 603979776 | bytes 3211264 | tf_op jit(solution)/shard_map/scbjz,ji->scbiz/dot_general | solution.py:74
  21.1 2.6 %add_bitcast_fusion = f32[8,3,128,128]{2,3,1,0:T(8,128)S(1)} fusion(f32[128,8,3,128]{0,3,2,1:T(8,128)S(1)} %fusion.2, f32[8,3,2,128,128]{4,3,2,1,0:T(8,128)S(1)} %bitcast.91, f32[256,128]{1,0:T(8,128)S(1)} %fusion.9), kind=kOutput, calls=%fused_computation.13 | convolution fusion | flops 604372992 | bytes 4784128 | tf_op jit(solution)/shard_map/scbjz,ji->scbiz/dot_general | solution.py:71
  23.9 4.3 %collective-permute-start.2 = (f32[8,3,128,64]{2,3,1,0:T(8,128)S(1)}, f32[8,3,128,64]{2,3,1,0:T(8,128)S(1)}, u32[]{:S(2)}, u32[]{:S(2)}) collective-permute-start(f32[8,3,128,64]{2,3,1,0:T(8,128)S(1)} %get-tuple-element.14), channel_id=1, source_target_pairs={{0,1},{1,2},{2,3},{3,4},{4,5},{5,6},{6,7},{7,8},{8,9},{9,10},{10,1... | collective-permute-start | bytes 2359304 | tf_op jit(solution)/shard_map/ppermute | solution.py:19
  28.2 10.8 %collective-permute-start.3 = (f32[8,3,128,64]{2,3,1,0:T(8,128)S(1)}, f32[8,3,128,64]{2,3,1,0:T(8,128)S(1)}, u32[]{:S(2)}, u32[]{:S(2)}) collective-permute-start(f32[8,3,128,64]{2,3,1,0:T(8,128)S(1)} %get-tuple-element.15), channel_id=1, source_target_pairs={{1,0},{2,1},{3,2},{4,3},{5,4},{6,5},{7,6},{8,7},{9,8},{10,9},{11,1... | collective-permute-start | bytes 2359304 | tf_op jit(solution)/shard_map/ppermute | solution.py:22
  39.0 16.3 %collective-permute-done.2 = f32[8,3,128,64]{2,3,1,0:T(8,128)S(1)} collective-permute-done((f32[8,3,128,64]{2,3,1,0:T(8,128)S(1)}, f32[8,3,128,64]{2,3,1,0:T(8,128)S(1)}, u32[]{:S(2)}, u32[]{:S(2)}) %collective-permute-start.2) | collective-permute-done | bytes 786464 | tf_op jit(solution)/shard_map/ppermute | solution.py:19
  55.3 1.5 %collective-permute-done.3 = f32[8,3,128,64]{2,3,1,0:T(8,128)S(1)} collective-permute-done((f32[8,3,128,64]{2,3,1,0:T(8,128)S(1)}, f32[8,3,128,64]{2,3,1,0:T(8,128)S(1)}, u32[]{:S(2)}, u32[]{:S(2)}) %collective-permute-start.3) | collective-permute-done | bytes 786464 | tf_op jit(solution)/shard_map/ppermute | solution.py:22
  56.8 0.3 pad_maximum_fusion.1
  57.1 1.5 %fusion = f32[8,3,128,128]{2,3,1,0:T(8,128)S(1)} fusion(f32[8,3,128,2,128]{2,4,3,1,0:T(8,128)S(1)} %bitcast.88, f32[256,128]{1,0:T(8,128)S(1)} %fusion.9), kind=kOutput, calls=%fused_computation.3 | convolution fusion | flops 603979776 | bytes 3211264 | tf_op jit(solution)/shard_map/dot_general | solution.py:62
  58.6 1.8 %fusion.18 = (f32[8,3,128]{2,1,0:T(4,128)S(1)}, f32[8,3,128]{2,1,0:T(4,128)S(1)}, f32[8,3,128,128]{2,3,1,0:T(8,128)S(1)}) fusion(f32[8,3,128,128]{2,3,1,0:T(8,128)S(1)} %fusion, f32[256,128]{1,0:T(8,128)S(1)} %fusion.9, f32[8,3,128,2,128]{2,4,3,1,0:T(8,128)S(1)} %bitcast.89), kind=kOutput, calls=%fused_computation.49 | convolution fusion | flops 605546496 | bytes 4808704 | tf_op jit(solution)/shard_map/dot_general | solution.py:61
  60.5 1.3 %broadcast_in_dim.8 = f32[32,1,6144]{2,1,0:T(1,128)} broadcast(f32[6144]{0:T(1024)S(1)} %pad_maximum_fusion.3), dimensions={2} | broadcast | bytes 811008 | tf_op jit(solution)/shard_map/broadcast_in_dim | solution.py:29
  61.7 7.5 %all-to-all-start = ((f32[32,1,6144]{2,1,0:T(1,128)}), f32[32,1,6144]{2,1,0:T(1,128)S(1)}, u32[]{:S(2)}, u32[]{:S(2)}) async-start(f32[32,1,6144]{2,1,0:T(1,128)} %broadcast_in_dim.8), calls=%async_computation | async-start | bytes 1572864 | tf_op jit(solution)/shard_map/all_to_all | solution.py:29
  69.3 23.3 %all-to-all-done = f32[32,1,6144]{2,1,0:T(1,128)S(1)} async-done(((f32[32,1,6144]{2,1,0:T(1,128)}), f32[32,1,6144]{2,1,0:T(1,128)S(1)}, u32[]{:S(2)}, u32[]{:S(2)}) %all-to-all-start) | async-done | bytes 786464 | tf_op jit(solution)/shard_map/all_to_all | solution.py:29
  92.5 0.5 reduce_sum.43
  93.1 0.2 subtract_divide_fusion
  93.3 0.4 copy-done.2
  93.7 0.2 multiply_add_fusion.1
  94.1 1.6 %copy.30 = f32[8,3,128,128]{3,2,1,0:T(8,128)} copy(f32[8,3,128,128]{2,3,1,0:T(8,128)S(1)} %pad_maximum_fusion.2) | data formatting | bytes 3145728 | tf_op jit(solution)/shard_map/stack | solution.py:94
  (18 shorter events, 0.5 us)
Async XLA Ops:
  0.0 18.2 %copy-start = (f32[8,3,128,128]{3,2,1,0:T(8,128)S(1)}, f32[8,3,128,128]{3,2,1,0:T(8,128)}, u32[]{:S(2)}) copy-start(f32[8,3,128,128]{3,2,1,0:T(8,128)} %param.3) | copy-start | bytes 4718596
  2.8 13.5 %collective-permute-start = (f32[8,3,64,128]{3,2,1,0:T(8,128)}, f32[8,3,64,128]{3,2,1,0:T(8,128)S(1)}, u32[]{:S(2)}, u32[]{:S(2)}) collective-permute-start(f32[8,3,64,128]{3,2,1,0:T(8,128)} %get-tuple-element.16), channel_id=1, source_target_pairs={{0,32},{32,64},{64,96},{96,128},{128,160},{160,192},{192,224},{224... | collective-permute-start | bytes 2359304 | tf_op jit(solution)/shard_map/ppermute | solution.py:19
  4.7 13.5 %collective-permute-start.1 = (f32[8,3,64,128]{3,2,1,0:T(8,128)}, f32[8,3,64,128]{3,2,1,0:T(8,128)S(1)}, u32[]{:S(2)}, u32[]{:S(2)}) collective-permute-start(f32[8,3,64,128]{3,2,1,0:T(8,128)} %get-tuple-element.17), channel_id=1, source_target_pairs={{32,0},{64,32},{96,64},{128,96},{160,128},{192,160},{224,192},{256... | collective-permute-start | bytes 2359304 | tf_op jit(solution)/shard_map/ppermute | solution.py:22
  23.9 31.4 %collective-permute-start.2 = (f32[8,3,128,64]{2,3,1,0:T(8,128)S(1)}, f32[8,3,128,64]{2,3,1,0:T(8,128)S(1)}, u32[]{:S(2)}, u32[]{:S(2)}) collective-permute-start(f32[8,3,128,64]{2,3,1,0:T(8,128)S(1)} %get-tuple-element.14), channel_id=1, source_target_pairs={{0,1},{1,2},{2,3},{3,4},{4,5},{5,6},{6,7},{7,8},{8,9},{9,10},{10,1... | collective-permute-start | bytes 2359304 | tf_op jit(solution)/shard_map/ppermute | solution.py:19
  28.2 28.6 %collective-permute-start.3 = (f32[8,3,128,64]{2,3,1,0:T(8,128)S(1)}, f32[8,3,128,64]{2,3,1,0:T(8,128)S(1)}, u32[]{:S(2)}, u32[]{:S(2)}) collective-permute-start(f32[8,3,128,64]{2,3,1,0:T(8,128)S(1)} %get-tuple-element.15), channel_id=1, source_target_pairs={{1,0},{2,1},{3,2},{4,3},{5,4},{6,5},{7,6},{8,7},{9,8},{10,9},{11,1... | collective-permute-start | bytes 2359304 | tf_op jit(solution)/shard_map/ppermute | solution.py:22
  60.4 8.8 %copy-start.1 = (f32[6,128]{1,0:T(8,128)S(1)}, f32[6,128]{1,0:T(8,128)}, u32[]{:S(2)}) copy-start(f32[6,128]{1,0:T(8,128)} %param.4) | copy-start | bytes 9220
  61.7 30.8 %all-to-all-start = ((f32[32,1,6144]{2,1,0:T(1,128)}), f32[32,1,6144]{2,1,0:T(1,128)S(1)}, u32[]{:S(2)}, u32[]{:S(2)}) async-start(f32[32,1,6144]{2,1,0:T(1,128)} %broadcast_in_dim.8), calls=%async_computation | async-start | bytes 1572864 | tf_op jit(solution)/shard_map/all_to_all | solution.py:29
  93.1 0.7 copy-start.2
where the time goes:
time: 96 us; the launch traced here: 95.7 us
  waiting for transfers between devices  49.4 us (51%)
  starting transfers between devices  28.1 us (29%)
  matrix products  8.62 us (9%)
  local copies, waits for them, and re-layouts  6.4 us (7%)
  other arithmetic  2.31 us (2%)
    all_to_all x1, waiting for transfers between devices, from_everyone(): lax.all_to_all(jnp.broadcast_to(x[None], (peers, *x.shape)), axis, 0, 0,...  23.3 us
    ppermute x2, waiting for transfers between devices, with_halo(): lax.ppermute(lax.slice_in_dim(block, block.shape[dim] - width, None, axis...  22.8 us
    ppermute x2, starting transfers between devices, with_halo(): lax.ppermute(lax.slice_in_dim(block, 0, width, axis=dim), axis, backward)  14.4 us
    all_to_all x1, starting transfers between devices, from_everyone(): lax.all_to_all(jnp.broadcast_to(x[None], (peers, *x.shape)), axis, 0, 0,...  7.47 us
    ppermute x2, starting transfers between devices, with_halo(): lax.ppermute(lax.slice_in_dim(block, block.shape[dim] - width, None, axis...  6.19 us
    ppermute x2, waiting for transfers between devices, with_halo(): lax.ppermute(lax.slice_in_dim(block, 0, width, axis=dim), axis, backward)  3.36 us
    slice x2, local copies, waits for them, and re-layouts, with_halo(): lax.slice_in_dim(block, block.shape[dim] - width, None, axis=dim)  2.98 us
    dot_general x1, matrix products, filter_rows(): jnp.einsum('scbjz,ji->scbiz', blocks[:, :, 1:], band[width:], precision=l...  2.66 us
  transfers between devices with their start and end apart: 5, of which 5 were waited for; matrix products, arithmetic and copies ran while one was open for 1% of the time, Pallas kernels for 0%

commit v1 on v0

v1 whole, which is shorter than its diff:
```python
import functools

import jax
import jax.numpy as jnp
import numpy as np
from jax import lax
from jax.experimental import pallas as pl
from jax.experimental.pallas import tpu as pltpu
from jax.sharding import PartitionSpec as P

H = 64
T = 128
EPS = 1e-06
NB = 12
F32 = jnp.float32
HI = lax.Precision.HIGHEST


def band():
    k = np.arange(-H, H + 1, dtype=np.float64)
    norm = np.sqrt(np.sum(np.exp(-np.pi * k * k / (H / 2.0) ** 2)))
    src = np.concatenate([np.arange(T), np.arange(-H, 0), np.arange(T, T + H)])
    lag = src[:, None] - np.arange(T)[None, :]
    val = np.exp(-np.pi * lag * lag / (2.0 * (H / 2.0) ** 2)) / norm
    return np.where(np.abs(lag) <= H, val, 0.0).astype(np.float32)


def lanes_low(shape):
    return lax.broadcasted_iota(jnp.int32, shape, len(shape) - 1) < H


def half_turn(v):
    return pltpu.roll(v, H, 1)


def edges(v):
    low = lanes_low((H, T))
    a, b = v[:H], v[H:]
    right = jnp.where(low, half_turn(a), b)
    left = jnp.where(low, a, half_turn(b))
    return right, left


def joined(hl, hr):
    low = lanes_low((H, T))
    return jnp.concatenate(
        [jnp.where(low, hl, half_turn(hr)), jnp.where(low, half_turn(hl), hr)], axis=0
    )


def dot(a, b):
    return jnp.dot(a, b, precision=HI, preferred_element_type=F32)


def pack_kernel(xb, xa, top, bottom, right, left):
    for p in range(xb.shape[0]):
        top[p] = xb[p, :H]
        bottom[p] = xb[p, H:]
    for p in range(xa.shape[0]):
        r, l = edges(xa[p])
        right[p] = r
        left[p] = l


def y_pass(bt, x, up, down):
    return dot(bt[:, :T], x) + dot(bt[:, T:], jnp.concatenate([up, down], axis=0))


def z_pass(b, x, hl, hr):
    return dot(x, b[:T]) + dot(joined(hl, hr), b[T:])


def y_first_kernel(bt, x, up, down, n, right, left):
    for p in range(x.shape[0]):
        v = y_pass(bt, x[p], up[p], down[p])
        n[p] = v
        r, l = edges(v)
        right[p] = r
        left[p] = l


def z_first_kernel(b, x, hl, hr, n, top, bottom):
    for p in range(x.shape[0]):
        v = z_pass(b, x[p], hl[p], hr[p])
        n[p] = v
        top[p] = v[:H]
        bottom[p] = v[H:]


def put_stats(acc, f, p, count):
    lane = lax.broadcasted_iota(jnp.int32, (T, T), 1)
    mean = jnp.sum(f, axis=1, keepdims=True) * (1.0 / T)
    c = f - mean
    second = jnp.sum(c * c, axis=1, keepdims=True)
    acc = jnp.where(lane == p, mean, acc)
    return jnp.where(lane == p + count, second, acc)


def z_last_kernel(b, x, hl, hr, f, st):
    count = x.shape[0]
    acc = jnp.zeros((T, T), F32)
    for p in range(count):
        v = z_pass(b, x[p], hl[p], hr[p])
        f[p] = v
        acc = put_stats(acc, v, p, count)
    st[...] = acc.T[: 2 * count]


def y_last_kernel(bt, x, up, down, f, st):
    count = x.shape[0]
    acc = jnp.zeros((T, T), F32)
    for p in range(count):
        v = y_pass(bt, x[p], up[p], down[p])
        f[p] = v
        acc = put_stats(acc, v, p, count)
    st[...] = acc.T[: 2 * count]


def final_kernel(fb, fa, sb, sa, stress, profile, out):
    steps = out.shape[0]
    s = stress[...]
    a11 = jnp.sqrt(s[0:1])
    a21 = s[3:4] / a11
    a22 = jnp.sqrt(s[1:2] - a21 * a21)
    a31 = s[4:5] / a11
    a32 = (s[5:6] - a21 * a31) / a22
    a33 = jnp.sqrt(s[2:3] - a31 * a31 - a32 * a32)
    prof = profile[...].reshape(1, T)
    done = 0
    for f, st in ((fb, sb), (fa, sa)):
        count = f.shape[0]
        parts = [st[q] for q in range(st.shape[0])]
        means = [q[:count] for q in parts]
        mean = sum(means) * (1.0 / len(parts))
        second = sum(q[count:] for q in parts)
        spread = sum((m - mean) * (m - mean) for m in means)
        per = 4096.0 / len(parts)
        var = (second + spread * per) * (1.0 / 4096.0)
        inv = 1.0 / jnp.sqrt(var + EPS)
        rows = []
        for k in range(count // 3):
            i0, i1, i2 = (inv[3 * k + c : 3 * k + c + 1] for c in range(3))
            rows += [a11 * i0, a21 * i0, a22 * i1, a31 * i0, a32 * i1, a33 * i2]
        table = jnp.concatenate(
            [mean] + rows + [prof], axis=0
        )
        pad = jnp.zeros((T - table.shape[0], T), F32)
        cols = jnp.concatenate([table, pad], axis=0).T
        pcol = cols[:, count + 2 * count : count + 2 * count + 1]
        for k in range(count // 3):
            g = [f[3 * k + c] - cols[:, 3 * k + c : 3 * k + c + 1] for c in range(3)]
            w = [cols[:, count + 6 * k + q : count + 6 * k + q + 1] for q in range(6)]
            out[done + k, 0] = pcol + w[0] * g[0]
            out[done + k, 1] = w[1] * g[0] + w[2] * g[1]
            out[done + k, 2] = w[3] * g[0] + w[4] * g[1] + w[5] * g[2]
        done += count // 3


def sds(*shape):
    return jax.ShapeDtypeStruct(shape, F32)


def planes(n, rows=T, off=0):
    return pl.BlockSpec((n, rows, T), lambda i: (i + off, 0, 0))


def whole(*shape):
    return pl.BlockSpec(shape, lambda i: (0,) * len(shape))


def shift(v, axis, d, periodic):
    n = lax.axis_size(axis)
    pairs = [(i, (i + d) % n) for i in range(n) if periodic or 0 <= i + d < n]
    return lax.ppermute(v, axis, pairs)


def groups(nx, nz):
    zs = [[x * nz + z for z in range(nz)] for x in range(nx)]
    xs = [[x * nz + z for x in range(nx)] for z in range(nz)]
    return zs, xs


def everyone(v, n, g):
    return lax.all_to_all(
        jnp.broadcast_to(v[None], (n, *v.shape)), "sp", 0, 0, axis_index_groups=g, tiled=True
    )


def merged(parts, counts, tiles):
    out, at = [], 0
    for c in counts:
        m, s = parts[:, at : at + c], parts[:, at + c : at + 2 * c]
        mean = jnp.mean(m, axis=0)
        sec = jnp.sum(s, axis=0) + tiles * T * jnp.sum((m - mean) ** 2, axis=0)
        out += [mean, sec]
        at += 2 * c
    return jnp.concatenate(out, axis=0)


def body(random_slabs, stress, profile):
    x = random_slabs.reshape(24, T, T)
    nb, na = NB, 24 - NB
    b = jnp.asarray(band())
    bt = jnp.asarray(np.ascontiguousarray(band().T))
    g = 3
    kb, ka = nb // g, na // g
    off = nb // ka
    top, bottom, right, left = pl.pallas_call(
        pack_kernel,
        grid=(g,),
        in_specs=[planes(kb), planes(ka, off=off)],
        out_specs=[planes(kb, H), planes(kb, H), planes(ka, H), planes(ka, H)],
        out_shape=[sds(nb, H, T), sds(nb, H, T), sds(na, H, T), sds(na, H, T)],
        name="pack",
    )(x, x)
    up_b = shift(bottom, "wn", 1, False)
    down_b = shift(top, "wn", -1, False)
    hl_a = shift(right, "sp", 1, True)
    hr_a = shift(left, "sp", -1, True)
    n_b, right_b, left_b = pl.pallas_call(
        y_first_kernel,
        grid=(g,),
        in_specs=[whole(T, 2 * T), planes(kb), planes(kb, H), planes(kb, H)],
        out_specs=[planes(kb), planes(kb, H), planes(kb, H)],
        out_shape=[sds(nb, T, T), sds(nb, H, T), sds(nb, H, T)],
        name="y_first",
    )(bt, x, up_b, down_b)
    hl_b = shift(right_b, "sp", 1, True)
    hr_b = shift(left_b, "sp", -1, True)
    n_a, top_a, bottom_a = pl.pallas_call(
        z_first_kernel,
        grid=(g,),
        in_specs=[whole(2 * T, T), planes(ka, off=off), planes(ka, H), planes(ka, H)],
        out_specs=[planes(ka), planes(ka, H), planes(ka, H)],
        out_shape=[sds(na, T, T), sds(na, H, T), sds(na, H, T)],
        name="z_first",
    )(b, x, hl_a, hr_a)
    up_a = shift(bottom_a, "wn", 1, False)
    down_a = shift(top_a, "wn", -1, False)
    f_b, s_b = pl.pallas_call(
        z_last_kernel,
        grid=(1,),
        in_specs=[whole(2 * T, T), planes(nb), planes(nb, H), planes(nb, H)],
        out_specs=[planes(nb), whole(2 * nb, T)],
        out_shape=[sds(nb, T, T), sds(2 * nb, T)],
        name="z_last",
    )(b, n_b, hl_b, hr_b)
    f_a, s_a = pl.pallas_call(
        y_last_kernel,
        grid=(1,),
        in_specs=[whole(T, 2 * T), planes(na), planes(na, H), planes(na, H)],
        out_specs=[planes(na), whole(2 * na, T)],
        out_shape=[sds(na, T, T), sds(2 * na, T)],
        name="y_last",
    )(bt, n_a, up_a, down_a)
    zs, xs = groups(4, 8)
    st = jnp.concatenate([s_b, s_a], axis=0)
    st = merged(everyone(st, 8, zs), (nb, na), 1)
    st = everyone(st, 4, xs)
    out = pl.pallas_call(
        final_kernel,
        out_shape=sds(8, 3, T, T),
        name="final",
    )(f_b, f_a, st[:, : 2 * nb], st[:, 2 * nb :], stress, profile)
    return out


def solution(mesh):
    return jax.shard_map(
        body,
        mesh=mesh,
        in_specs=(P(None, None, "wn", "sp"), P(None, "wn"), P("wn")),
        out_specs=P(None, None, "wn", "sp"),
        check_vma=False,
    )
```

time: 96 us -> 98.9 us (1.030)
  the two profiles are of different devices: /device:TPU:48 before, /device:TPU:24 now
where the time goes in v1:
time: 98.9 us; the launch traced here: 98.2 us
  starting transfers between devices  35.7 us (36%)
  blocking collectives  25 us (25%)
  Pallas kernels  24.1 us (24%)
  waiting for transfers between devices  7.99 us (8%)
  local copies, waits for them, and re-layouts  4.53 us (5%)
    ppermute x8, starting transfers between devices, shift(): return lax.ppermute(v, axis, pairs)  35.7 us
    all_to_all x2, blocking collectives, everyone(): lax.all_to_all(jnp.broadcast_to(v[None], (n, *v.shape)), 'sp', 0, 0, axis...  25 us
    ppermute x8, waiting for transfers between devices, shift(): return lax.ppermute(v, axis, pairs)  7.99 us
    pallas_call x1, Pallas kernels, body(): pl.pallas_call(z_first_kernel, grid=(g,), in_specs=[whole(2 * T, T), plan...  4.5 us
    pallas_call x1, Pallas kernels, body(): pl.pallas_call(y_first_kernel, grid=(g,), in_specs=[whole(T, 2 * T), plan...  4.38 us
    pallas_call x1, Pallas kernels, body(): pl.pallas_call(final_kernel, out_shape=sds(8, 3, T, T), name='final')  4.19 us
    pallas_call x1, Pallas kernels, body(): pl.pallas_call(z_last_kernel, grid=(1,), in_specs=[whole(2 * T, T), plane...  3.89 us
    unnamed x18, local copies, waits for them, and re-layouts  3.85 us
  transfers between devices with their start and end apart: 8, of which 4 were waited for; matrix products, arithmetic and copies ran while one was open for 0% of the time, Pallas kernels for 13%

profile of v1, /device:TPU:24, one launch (start us, length us, event | category | flops | bytes accessed | tf_op | source)
XLA Modules:
  0.0 98.2 jit_solution(8896608014046421484)
XLA Ops:
  0.0 3.4 %pack.1 = (f32[12,64,128]{2,1,0:T(8,128)}, f32[12,64,128]{2,1,0:T(8,128)}, f32[12,64,128]{2,1,0:T(8,128)}, f32[12,64,128]{2,1,0:T(8,128)}) custom-call(f32[24,128,128]{2,1,0:T(8,128)} %bitcast.1, f32[24,128,128]{2,1,0:T(8,128)} %bitcast.2), custom_call_target="tpu_custom_call" | custom-call | tf_op jit(solution)/shard_map/pack/pallas_call | solution.py:208
  3.4 4.3 %collective-permute-start.4 = (f32[12,64,128]{2,1,0:T(8,128)}, f32[12,64,128]{2,1,0:T(8,128)S(1)}, u32[]{:S(2)}, u32[]{:S(2)}) collective-permute-start(f32[12,64,128]{2,1,0:T(8,128)} %get-tuple-element.25), channel_id=1, source_target_pairs={{0,1},{1,2},{2,3},{3,4},{4,5},{5,6},{6,7},{7,8},{8,9},{9,10},{10,1... | collective-permute-start | bytes 1179656 | tf_op jit(solution)/shard_map/ppermute | solution.py:174
  7.7 10.8 %collective-permute-start.5 = (f32[12,64,128]{2,1,0:T(8,128)}, f32[12,64,128]{2,1,0:T(8,128)S(1)}, u32[]{:S(2)}, u32[]{:S(2)}) collective-permute-start(f32[12,64,128]{2,1,0:T(8,128)} %get-tuple-element.26), channel_id=1, source_target_pairs={{0,31},{1,0},{2,1},{3,2},{4,3},{5,4},{6,5},{7,6},{8,7},{9,8},{10,9... | collective-permute-start | bytes 1179656 | tf_op jit(solution)/shard_map/ppermute | solution.py:174
  18.4 1.9 %collective-permute-start = (f32[12,64,128]{2,1,0:T(8,128)}, f32[12,64,128]{2,1,0:T(8,128)S(1)}, u32[]{:S(2)}, u32[]{:S(2)}) collective-permute-start(f32[12,64,128]{2,1,0:T(8,128)} %get-tuple-element.19), channel_id=1, source_target_pairs={{0,32},{32,64},{64,96},{96,128},{128,160},{160,192},{192,224},{224... | collective-permute-start | bytes 1179656 | tf_op jit(solution)/shard_map/ppermute | solution.py:174
  20.4 3.6 %collective-permute-start.1 = (f32[12,64,128]{2,1,0:T(8,128)}, f32[12,64,128]{2,1,0:T(8,128)S(1)}, u32[]{:S(2)}, u32[]{:S(2)}) collective-permute-start(f32[12,64,128]{2,1,0:T(8,128)} %get-tuple-element.20), channel_id=1, source_target_pairs={{32,0},{64,32},{96,64},{128,96},{160,128},{192,160},{224,192},{256... | collective-permute-start | bytes 1179656 | tf_op jit(solution)/shard_map/ppermute | solution.py:174
  24.0 1.8 %collective-permute-done.4.hl = f32[12,64,128]{2,1,0:T(8,128)S(1)} collective-permute-done((f32[12,64,128]{2,1,0:T(8,128)}, f32[12,64,128]{2,1,0:T(8,128)S(1)}, u32[]{:S(2)}, u32[]{:S(2)}) %collective-permute-start.4) | collective-permute-done | bytes 393248 | tf_op jit(solution)/shard_map/ppermute | solution.py:174
  25.8 1.3 %collective-permute-done.5.hr = f32[12,64,128]{2,1,0:T(8,128)S(1)} collective-permute-done((f32[12,64,128]{2,1,0:T(8,128)}, f32[12,64,128]{2,1,0:T(8,128)S(1)}, u32[]{:S(2)}, u32[]{:S(2)}) %collective-permute-start.5) | collective-permute-done | bytes 393248 | tf_op jit(solution)/shard_map/ppermute | solution.py:174
  27.1 0.8 copy-done.3
  27.9 4.5 %z_first.1 = (f32[12,128,128]{2,1,0:T(8,128)}, f32[12,64,128]{2,1,0:T(8,128)}, f32[12,64,128]{2,1,0:T(8,128)}) custom-call(f32[256,128]{1,0:T(8,128)} %constant.12.clone.b, f32[24,128,128]{2,1,0:T(8,128)} %bitcast.3, f32[12,64,128]{2,1,0:T(8,128)} %copy-done.2, f32[12,64,128]{2,1,0:T(8,128)} %copy-done.3), custom_call_target="tpu_custom_call" | custom-call | tf_op jit(solution)/shard_map/z_first/pallas_call | solution.py:230
  32.4 1.9 %collective-permute-start.6 = (f32[12,64,128]{2,1,0:T(8,128)}, f32[12,64,128]{2,1,0:T(8,128)S(1)}, u32[]{:S(2)}, u32[]{:S(2)}) collective-permute-start(f32[12,64,128]{2,1,0:T(8,128)} %get-tuple-element.28), channel_id=1, source_target_pairs={{0,32},{32,64},{64,96},{96,128},{128,160},{160,192},{192,224},{224... | collective-permute-start | bytes 1179656 | tf_op jit(solution)/shard_map/ppermute | solution.py:174
  34.3 3.6 %collective-permute-start.7 = (f32[12,64,128]{2,1,0:T(8,128)}, f32[12,64,128]{2,1,0:T(8,128)S(1)}, u32[]{:S(2)}, u32[]{:S(2)}) collective-permute-start(f32[12,64,128]{2,1,0:T(8,128)} %get-tuple-element.29), channel_id=1, source_target_pairs={{32,0},{64,32},{96,64},{128,96},{160,128},{192,160},{224,192},{256... | collective-permute-start | bytes 1179656 | tf_op jit(solution)/shard_map/ppermute | solution.py:174
  38.0 0.7 copy-done
  38.7 0.7 copy-done.1
  39.5 4.4 %y_first.1 = (f32[12,128,128]{2,1,0:T(8,128)}, f32[12,64,128]{2,1,0:T(8,128)}, f32[12,64,128]{2,1,0:T(8,128)}) custom-call(f32[128,256]{1,0:T(8,128)} %constant.13.clone.bt, f32[24,128,128]{2,1,0:T(8,128)} %bitcast.4, f32[12,64,128]{2,1,0:T(8,128)} %copy-done, f32[12,64,128]{2,1,0:T(8,128)} %copy-done.1), custom_call_target="tpu_custom_call" | custom-call | tf_op jit(solution)/shard_map/y_first/pallas_call | solution.py:220
  43.8 1.9 %collective-permute-start.2 = (f32[12,64,128]{2,1,0:T(8,128)}, f32[12,64,128]{2,1,0:T(8,128)S(1)}, u32[]{:S(2)}, u32[]{:S(2)}) collective-permute-start(f32[12,64,128]{2,1,0:T(8,128)} %get-tuple-element.22), channel_id=1, source_target_pairs={{0,1},{1,2},{2,3},{3,4},{4,5},{5,6},{6,7},{7,8},{8,9},{9,10},{10,1... | collective-permute-start | bytes 1179656 | tf_op jit(solution)/shard_map/ppermute | solution.py:174
  45.7 7.6 %collective-permute-start.3 = (f32[12,64,128]{2,1,0:T(8,128)}, f32[12,64,128]{2,1,0:T(8,128)S(1)}, u32[]{:S(2)}, u32[]{:S(2)}) collective-permute-start(f32[12,64,128]{2,1,0:T(8,128)} %get-tuple-element.23), channel_id=1, source_target_pairs={{0,31},{1,0},{2,1},{3,2},{4,3},{5,4},{6,5},{7,6},{8,7},{9,8},{10,9... | collective-permute-start | bytes 1179656 | tf_op jit(solution)/shard_map/ppermute | solution.py:174
  54.2 3.8 %y_last.1 = (f32[12,128,128]{2,1,0:T(8,128)}, f32[24,128]{1,0:T(8,128)}) custom-call(f32[128,256]{1,0:T(8,128)} %constant.13.clone.bt, f32[12,128,128]{2,1,0:T(8,128)} %get-tuple-element.27.x, f32[12,64,128]{2,1,0:T(8,128)} %copy-done.4, f32[12,64,128]{2,1,0:T(8,128)} %copy-done.5), custom_call_target="tpu_custom_call" | custom-call | tf_op jit(solution)/shard_map/y_last/pallas_call | solution.py:248
  58.0 3.1 %collective-permute-done.2.hl = f32[12,64,128]{2,1,0:T(8,128)S(1)} collective-permute-done((f32[12,64,128]{2,1,0:T(8,128)}, f32[12,64,128]{2,1,0:T(8,128)S(1)}, u32[]{:S(2)}, u32[]{:S(2)}) %collective-permute-start.2) | collective-permute-done | bytes 393248 | tf_op jit(solution)/shard_map/ppermute | solution.py:174
  61.1 1.8 %collective-permute-done.3.hr = f32[12,64,128]{2,1,0:T(8,128)S(1)} collective-permute-done((f32[12,64,128]{2,1,0:T(8,128)}, f32[12,64,128]{2,1,0:T(8,128)S(1)}, u32[]{:S(2)}, u32[]{:S(2)}) %collective-permute-start.3) | collective-permute-done | bytes 393248 | tf_op jit(solution)/shard_map/ppermute | solution.py:174
  63.0 0.7 copy-done.7
  63.7 3.9 %z_last.1 = (f32[12,128,128]{2,1,0:T(8,128)}, f32[24,128]{1,0:T(8,128)}) custom-call(f32[256,128]{1,0:T(8,128)} %constant.12.clone.b, f32[12,128,128]{2,1,0:T(8,128)} %get-tuple-element.21.x, f32[12,64,128]{2,1,0:T(8,128)} %copy-done.6, f32[12,64,128]{2,1,0:T(8,128)} %copy-done.7), custom_call_target="tpu_custom_call" | custom-call | tf_op jit(solution)/shard_map/z_last/pallas_call | solution.py:240
  68.3 13.6 %all_to_all.10 = f32[8,48,128]{2,1,0:T(8,128)S(1)} all-to-all(f32[8,48,128]{2,1,0:T(8,128)S(1)} %broadcast_in_dim.4), channel_id=1, replica_groups={{0,1,2,3,4,5,6,7},{8,9,10,11,12,13,14,15},{16,17,18,19,20,21,22,23},{24..., dimensions={0} | all-to-all | bytes 393216 | tf_op jit(solution)/shard_map/all_to_all | solution.py:184
  82.1 11.3 %all_to_all.11 = f32[4,48,128]{2,1,0:T(8,128)S(1)} all-to-all(f32[4,48,128]{2,1,0:T(8,128)S(1)} %broadcast_in_dim.5), channel_id=1, replica_groups={{0,8,16,24},{1,9,17,25},{2,10,18,26},{3,11,19,27},{4,12,20,28},{5,13,21..., dimensions={0} | all-to-all | bytes 196608 | tf_op jit(solution)/shard_map/all_to_all | solution.py:184
  94.1 4.2 %final.1 = f32[8,3,128,128]{3,2,1,0:T(8,128)} custom-call(f32[12,128,128]{2,1,0:T(8,128)} %get-tuple-element.24.fb, f32[12,128,128]{2,1,0:T(8,128)} %get-tuple-element.30.fa, f32[4,24,128]{2,1,0:T(8,128)} %get-tuple-element.40.sb, f32[4,24,128]{2,1,0:T(8,128)} %get-tuple-element.39.sa, f32[6,128]{1,0:T(8,128)} %stress.1, f32[128]{0:T(128)} %profile.1), custom_call_target="tpu_custom_call" | custom-call | tf_op jit(solution)/shard_map/final/pallas_call | solution.py:260
  (28 shorter events, 2.3 us)
Async XLA Ops:
  3.4 22.4 %collective-permute-start.4 = (f32[12,64,128]{2,1,0:T(8,128)}, f32[12,64,128]{2,1,0:T(8,128)S(1)}, u32[]{:S(2)}, u32[]{:S(2)}) collective-permute-start(f32[12,64,128]{2,1,0:T(8,128)} %get-tuple-element.25), channel_id=1, source_target_pairs={{0,1},{1,2},{2,3},{3,4},{4,5},{5,6},{6,7},{7,8},{8,9},{9,10},{10,1... | collective-permute-start | bytes 1179656 | tf_op jit(solution)/shard_map/ppermute | solution.py:174
  7.7 19.5 %collective-permute-start.5 = (f32[12,64,128]{2,1,0:T(8,128)}, f32[12,64,128]{2,1,0:T(8,128)S(1)}, u32[]{:S(2)}, u32[]{:S(2)}) collective-permute-start(f32[12,64,128]{2,1,0:T(8,128)} %get-tuple-element.26), channel_id=1, source_target_pairs={{0,31},{1,0},{2,1},{3,2},{4,3},{5,4},{6,5},{7,6},{8,7},{9,8},{10,9... | collective-permute-start | bytes 1179656 | tf_op jit(solution)/shard_map/ppermute | solution.py:174
  18.4 19.5 %collective-permute-start = (f32[12,64,128]{2,1,0:T(8,128)}, f32[12,64,128]{2,1,0:T(8,128)S(1)}, u32[]{:S(2)}, u32[]{:S(2)}) collective-permute-start(f32[12,64,128]{2,1,0:T(8,128)} %get-tuple-element.19), channel_id=1, source_target_pairs={{0,32},{32,64},{64,96},{96,128},{128,160},{160,192},{192,224},{224... | collective-permute-start | bytes 1179656 | tf_op jit(solution)/shard_map/ppermute | solution.py:174
  20.4 17.6 %collective-permute-start.1 = (f32[12,64,128]{2,1,0:T(8,128)}, f32[12,64,128]{2,1,0:T(8,128)S(1)}, u32[]{:S(2)}, u32[]{:S(2)}) collective-permute-start(f32[12,64,128]{2,1,0:T(8,128)} %get-tuple-element.20), channel_id=1, source_target_pairs={{32,0},{64,32},{96,64},{128,96},{160,128},{192,160},{224,192},{256... | collective-permute-start | bytes 1179656 | tf_op jit(solution)/shard_map/ppermute | solution.py:174
  25.8 1.3 %copy-start.2 = (f32[12,64,128]{2,1,0:T(8,128)}, f32[12,64,128]{2,1,0:T(8,128)S(1)}, u32[]{:S(2)}) copy-start(f32[12,64,128]{2,1,0:T(8,128)S(1)} %collective-permute-done.4.hl) | copy-start | bytes 1179652
  27.1 0.8 copy-start.3
  32.4 21.0 %collective-permute-start.6 = (f32[12,64,128]{2,1,0:T(8,128)}, f32[12,64,128]{2,1,0:T(8,128)S(1)}, u32[]{:S(2)}, u32[]{:S(2)}) collective-permute-start(f32[12,64,128]{2,1,0:T(8,128)} %get-tuple-element.28), channel_id=1, source_target_pairs={{0,32},{32,64},{64,96},{96,128},{128,160},{160,192},{192,224},{224... | collective-permute-start | bytes 1179656 | tf_op jit(solution)/shard_map/ppermute | solution.py:174
  34.3 19.1 %collective-permute-start.7 = (f32[12,64,128]{2,1,0:T(8,128)}, f32[12,64,128]{2,1,0:T(8,128)S(1)}, u32[]{:S(2)}, u32[]{:S(2)}) collective-permute-start(f32[12,64,128]{2,1,0:T(8,128)} %get-tuple-element.29), channel_id=1, source_target_pairs={{32,0},{64,32},{96,64},{128,96},{160,128},{192,160},{224,192},{256... | collective-permute-start | bytes 1179656 | tf_op jit(solution)/shard_map/ppermute | solution.py:174
  37.9 0.8 copy-start
  38.7 0.7 copy-start.1
  43.8 17.3 %collective-permute-start.2 = (f32[12,64,128]{2,1,0:T(8,128)}, f32[12,64,128]{2,1,0:T(8,128)S(1)}, u32[]{:S(2)}, u32[]{:S(2)}) collective-permute-start(f32[12,64,128]{2,1,0:T(8,128)} %get-tuple-element.22), channel_id=1, source_target_pairs={{0,1},{1,2},{2,3},{3,4},{4,5},{5,6},{6,7},{7,8},{8,9},{9,10},{10,1... | collective-permute-start | bytes 1179656 | tf_op jit(solution)/shard_map/ppermute | solution.py:174
  45.7 17.2 %collective-permute-start.3 = (f32[12,64,128]{2,1,0:T(8,128)}, f32[12,64,128]{2,1,0:T(8,128)S(1)}, u32[]{:S(2)}, u32[]{:S(2)}) collective-permute-start(f32[12,64,128]{2,1,0:T(8,128)} %get-tuple-element.23), channel_id=1, source_target_pairs={{0,31},{1,0},{2,1},{3,2},{4,3},{5,4},{6,5},{7,6},{8,7},{9,8},{10,9... | collective-permute-start | bytes 1179656 | tf_op jit(solution)/shard_map/ppermute | solution.py:174
  53.4 0.8 copy-start.4
  53.4 0.9 copy-start.5
  58.0 9.5 %copy-start.8 = (f32[24,128]{1,0:T(8,128)S(1)}, f32[24,128]{1,0:T(8,128)}, u32[]{:S(2)}) copy-start(f32[24,128]{1,0:T(8,128)} %get-tuple-element.32) | copy-start | bytes 36868
  61.1 1.8 %copy-start.6 = (f32[12,64,128]{2,1,0:T(8,128)}, f32[12,64,128]{2,1,0:T(8,128)S(1)}, u32[]{:S(2)}) copy-start(f32[12,64,128]{2,1,0:T(8,128)S(1)} %collective-permute-done.2.hl) | copy-start | bytes 1179652
  62.9 0.8 copy-start.7

commit v2 on v0

v2 whole, which is shorter than its diff:
```python
import jax
import jax.numpy as jnp
import numpy as np
from jax import lax
from jax.experimental import pallas as pl
from jax.experimental.pallas import tpu as pltpu
from jax.sharding import PartitionSpec as P


H = 64
T = 128
EPS = 1e-06
NB = 9
NA = 24 - NB
F32 = jnp.float32
BF = jnp.bfloat16


def band():
    k = np.arange(-H, H + 1, dtype=np.float64)
    norm = np.sqrt(np.sum(np.exp(-np.pi * k * k / (H / 2.0) ** 2)))
    src = np.concatenate([np.arange(T), np.arange(-H, 0), np.arange(T, T + H)])
    lag = src[:, None] - np.arange(T)[None, :]
    val = np.exp(-np.pi * lag * lag / (2.0 * (H / 2.0) ** 2)) / norm
    return np.where(np.abs(lag) <= H, val, 0.0).astype(np.float32)


def pieces(v):
    h = v.astype(BF)
    r = v - h.astype(F32)
    m = r.astype(BF)
    return h, m, (r - m.astype(F32)).astype(BF)


def bands():
    b = band()
    h = b.astype(BF)
    m = (b - h.astype(np.float32)).astype(BF)
    low = (b - h.astype(np.float32) - m.astype(np.float32)).astype(BF)
    across = np.concatenate([h, m, low], axis=1)
    return np.ascontiguousarray(across), np.ascontiguousarray(across.T)


def lanes_low(shape):
    return lax.broadcasted_iota(jnp.int32, shape, len(shape) - 1) < H


def half_turn(v):
    return pltpu.roll(v, H, 1)


def edges(v, even):
    low = lanes_low((H, T))
    a, b = v[:H], v[H:]
    right = jnp.where(low, half_turn(a), b)
    left = jnp.where(low, a, half_turn(b))
    return jnp.where(even, right, left), jnp.where(even, left, right)


def joined(re, ro, even):
    low = lanes_low((H, T))
    hl = jnp.where(even, ro, re)
    hr = jnp.where(even, re, ro)
    return jnp.concatenate(
        [jnp.where(low, hl, half_turn(hr)), jnp.where(low, half_turn(hl), hr)], axis=0
    )


def mm(a, b):
    return jnp.dot(a, b, preferred_element_type=F32)


def y_pass(bt, x, re, ro, even):
    cols = []
    for v, e, o in zip(x, re, ro):
        up = jnp.where(even, o, e)
        down = jnp.where(even, e, o)
        cols.append(jnp.concatenate([v, up, down], axis=0))
    w = cols[0] if len(cols) == 1 else jnp.concatenate(cols, axis=1)
    h, m, low = pieces(w)
    p = mm(bt, h)
    q = mm(bt[: 2 * T], m)
    r = mm(bt[:T], low)
    out = p[:T] + ((p[T : 2 * T] + q[:T]) + (p[2 * T :] + (q[T:] + r)))
    return [out[:, T * i : T * (i + 1)] for i in range(len(cols))]


def z_pass(b, x, re, ro, even):
    rows = [
        jnp.concatenate([v, joined(e, o, even)], axis=1) for v, e, o in zip(x, re, ro)
    ]
    w = rows[0] if len(rows) == 1 else jnp.concatenate(rows, axis=0)
    h, m, low = pieces(w)
    p = mm(h, b)
    q = mm(m, b[:, : 2 * T])
    r = mm(low, b[:, :T])
    out = p[:, :T] + (
        (p[:, T : 2 * T] + q[:, :T]) + (p[:, 2 * T :] + (q[:, T:] + r))
    )
    return [out[T * i : T * (i + 1)] for i in range(len(rows))]


def cuts(n, step):
    return [range(i, min(i + step, n)) for i in range(0, n, step)]


def pack_kernel(par, x, yo, ye, zo, ze):
    off = pl.multiple_of(par[1] * H, H)
    opp = pl.multiple_of(H - off, H)
    zeven = par[0] == 0
    for p in range(NB):
        yo[p] = x[p, pl.ds(off, H)]
        ye[p] = x[p, pl.ds(opp, H)]
    for p in range(NA):
        e, o = edges(x[NB + p], zeven)
        ze[p] = e
        zo[p] = o


def y_first_kernel(par, bt, x, ro, re, n, zo, ze):
    zeven, yeven = par[0] == 0, par[1] == 0
    for c in cuts(NB, 2):
        got = y_pass(bt[...], [x[p] for p in c], [re[p] for p in c], [ro[p] for p in c], yeven)
        for p, v in zip(c, got):
            n[p] = v
            e, o = edges(v, zeven)
            ze[p] = e
            zo[p] = o


def z_first_kernel(par, b, x, ro, re, n, yo, ye):
    off = par[1]
    zeven, yeven = par[0] == 0, off == 0
    for c in cuts(NA, 3):
        got = z_pass(
            b[...], [x[NB + p] for p in c], [re[p] for p in c], [ro[p] for p in c], zeven
        )
        for p, v in zip(c, got):
            n[p] = v
            yo[p] = jnp.where(yeven, v[:H], v[H:])
            ye[p] = jnp.where(yeven, v[H:], v[:H])


def put_stats(acc, f, p):
    lane = lax.broadcasted_iota(jnp.int32, (T, T), 1)
    mean = jnp.sum(f, axis=1, keepdims=True) * (1.0 / T)
    c = f - mean
    second = jnp.sum(c * c, axis=1, keepdims=True)
    acc = jnp.where(lane == p, mean, acc)
    return jnp.where(lane == p + 24, second, acc)


def z_last_kernel(par, b, x, ro, re, f, st):
    zeven = par[0] == 0
    acc = jnp.zeros((T, T), F32)
    for c in cuts(NB, 3):
        got = z_pass(b[...], [x[p] for p in c], [re[p] for p in c], [ro[p] for p in c], zeven)
        for p, v in zip(c, got):
            f[p] = v
            acc = put_stats(acc, v, p)
    st[...] = acc


def y_last_kernel(par, bt, x, ro, re, acc_b, f, st):
    yeven = par[1] == 0
    acc = acc_b[...]
    for c in cuts(NA, 2):
        got = y_pass(bt[...], [x[p] for p in c], [re[p] for p in c], [ro[p] for p in c], yeven)
        for p, v in zip(c, got):
            f[p] = v
            acc = put_stats(acc, v, p + NB)
    flat = acc.T[:48]
    for q in range(st.shape[0]):
        st[q] = flat


def merge(st, tiles):
    n = st.shape[0]
    parts = [st[q] for q in range(n)]
    mean = sum(q[:24] for q in parts) * (1.0 / n)
    second = sum(q[24:] for q in parts)
    spread = sum((q[:24] - mean) * (q[:24] - mean) for q in parts)
    return mean, second + spread * float(tiles * T)


def mid_kernel(st, out):
    mean, second = merge(st, 1)
    for q in range(out.shape[0]):
        out[q, :24] = mean
        out[q, 24:] = second


def final_kernel(fb, fa, st, stress, profile, out, buf, sems):
    mean, second = merge(st, 8)
    inv = 1.0 / jnp.sqrt(second * (1.0 / 4096.0) + EPS)
    s = stress[...]
    a11 = jnp.sqrt(s[0:1])
    a21 = s[3:4] / a11
    a22 = jnp.sqrt(s[1:2] - a21 * a21)
    a31 = s[4:5] / a11
    a32 = (s[5:6] - a21 * a31) / a22
    a33 = jnp.sqrt(s[2:3] - a31 * a31 - a32 * a32)
    prof = profile[...].reshape(1, T)
    rows = []
    for k in range(8):
        i0, i1, i2 = (inv[3 * k + c : 3 * k + c + 1] for c in range(3))
        rows += [a11 * i0, a21 * i0, a22 * i1, a31 * i0, a32 * i1, a33 * i2]
    table = jnp.concatenate([mean] + rows + [prof], axis=0)
    cols = jnp.concatenate([table, jnp.zeros((T - 73, T), F32)], axis=0).T
    pcol = cols[:, 72:73]
    copies = []
    for k in range(8):
        g = []
        for c in range(3):
            p = 3 * k + c
            v = fb[p] if p < NB else fa[p - NB]
            g.append(v - cols[:, p : p + 1])
        w = [cols[:, 24 + 6 * k + q : 25 + 6 * k + q] for q in range(6)]
        buf[k, 0] = pcol + w[0] * g[0]
        buf[k, 1] = w[1] * g[0] + w[2] * g[1]
        buf[k, 2] = w[3] * g[0] + w[4] * g[1] + w[5] * g[2]
        copy = pltpu.make_async_copy(buf.at[k], out.at[k], sems.at[k])
        copy.start()
        copies.append(copy)
    for copy in copies:
        copy.wait()


def call(kernel, ins, outs, scratch=(), hbm_out=False):
    smem = pl.BlockSpec(memory_space=pltpu.SMEM)
    vmem = pl.BlockSpec(memory_space=pltpu.VMEM)
    args, specs = [], []
    for a in ins:
        if a.dtype == jnp.int32:
            args.append(a)
            specs.append(smem)
        else:
            args.append(pltpu.with_memory_space_constraint(a, pltpu.VMEM))
            specs.append(vmem)
    if hbm_out:
        shapes = [jax.ShapeDtypeStruct(s, F32) for s in outs]
        out_specs = [pl.BlockSpec(memory_space=pl.ANY) for s in outs]
    else:
        shapes = [pltpu.VMEM(s, F32) for s in outs]
        out_specs = [vmem for s in outs]
    return pl.pallas_call(
        kernel,
        in_specs=specs,
        out_specs=out_specs,
        out_shape=shapes,
        scratch_shapes=list(scratch),
        compiler_params=pltpu.CompilerParams(vmem_limit_bytes=24 << 20),
    )(*args)


def swap(v, axis, odd, periodic):
    n = lax.axis_size(axis)
    pairs = []
    for i in range(odd, n, 2):
        j = (i + 1) % n
        if periodic or j > i:
            pairs += [(i, j), (j, i)]
    return lax.ppermute(v, axis, pairs)


def groups(nx, nz):
    zs = [[x * nz + z for z in range(nz)] for x in range(nx)]
    xs = [[x * nz + z for x in range(nx)] for z in range(nz)]
    return zs, xs


def run(random_slabs, stress, profile):
    x = random_slabs.reshape(24, T, T)
    par = jnp.stack([lax.axis_index("sp") % 2, lax.axis_index("wn") % 2]).astype(jnp.int32)
    b, bt = (jnp.asarray(v) for v in bands())
    hb, ha = (NB, H, T), (NA, H, T)
    fb, fa = (NB, T, T), (NA, T, T)
    yo, ye, zo, ze = call(pack_kernel, [par, x], [hb, hb, ha, ha])
    yo = swap(yo, "wn", 1, False)
    ye = swap(ye, "wn", 0, False)
    zo = swap(zo, "sp", 1, True)
    ze = swap(ze, "sp", 0, True)
    n_b, zo_b, ze_b = call(y_first_kernel, [par, bt, x, yo, ye], [fb, hb, hb])
    zo_b = swap(zo_b, "sp", 1, True)
    ze_b = swap(ze_b, "sp", 0, True)
    n_a, yo_a, ye_a = call(z_first_kernel, [par, b, x, zo, ze], [fa, ha, ha])
    yo_a = swap(yo_a, "wn", 1, False)
    ye_a = swap(ye_a, "wn", 0, False)
    f_b, s_b = call(z_last_kernel, [par, b, n_b, zo_b, ze_b], [fb, (T, T)])
    zs, xs = groups(4, 8)
    f_a, st = call(y_last_kernel, [par, bt, n_a, yo_a, ye_a, s_b], [fa, (8, 48, T)])
    st = lax.all_to_all(st, "sp", 0, 0, axis_index_groups=zs, tiled=True)
    (st,) = call(mid_kernel, [st], [(4, 48, T)])
    st = lax.all_to_all(st, "sp", 0, 0, axis_index_groups=xs, tiled=True)
    (out,) = call(
        final_kernel,
        [f_b, f_a, st, stress, profile],
        [(8, 3, T, T)],
        scratch=[pltpu.VMEM((8, 3, T, T), F32), pltpu.SemaphoreType.DMA((8,))],
        hbm_out=True,
    )
    return out


def solution(mesh):
    return jax.shard_map(
        run,
        mesh=mesh,
        in_specs=(P(None, None, "wn", "sp"), P(None, "wn"), P("wn")),
        out_specs=P(None, None, "wn", "sp"),
        check_vma=False,
    )
```

time: 96 us -> 82.7 us (0.86)
  the two profiles are of different devices: /device:TPU:48 before, /device:TPU:24 now
where the time goes in v2:
time: 82.7 us; the launch traced here: 82.3 us
  starting transfers between devices  34.1 us (41%)
  blocking collectives  22 us (27%)
  waiting for transfers between devices  14.6 us (18%)
  Pallas kernels  9.95 us (12%)
  local copies, waits for them, and re-layouts  1.43 us (2%)
    ppermute x8, starting transfers between devices, swap(): return lax.ppermute(v, axis, pairs)  34.1 us
    ppermute x8, waiting for transfers between devices, swap(): return lax.ppermute(v, axis, pairs)  14.6 us
    all_to_all x1, blocking collectives, run(): st = lax.all_to_all(st, 'sp', 0, 0, axis_index_groups=zs, tiled=True)  12.5 us
    pallas_call x7, Pallas kernels, call(): pl.pallas_call(kernel, in_specs=specs, out_specs=out_specs, out_shape=sha...  9.95 us
    all_to_all x1, blocking collectives, run(): st = lax.all_to_all(st, 'sp', 0, 0, axis_index_groups=xs, tiled=True)  9.48 us
  transfers between devices with their start and end apart: 8, of which 3 were waited for; matrix products, arithmetic and copies ran while one was open for 0% of the time, Pallas kernels for 6%

profile of v2, /device:TPU:24, one launch (start us, length us, event | category | flops | bytes accessed | tf_op | source)
XLA Modules:
  0.0 82.3 jit_solution(18421815530977724426)
XLA Ops:
  0.0 0.1 pad_add_fusion.par
  0.1 1.4 %copy-done = f32[8,3,128,128]{3,2,1,0:T(8,128)S(1)} copy-done((f32[8,3,128,128]{3,2,1,0:T(8,128)S(1)}, f32[8,3,128,128]{3,2,1,0:T(8,128)}, u32[]{:S(2)}) %copy-start) | copy-done | bytes 1572888
  1.5 0.9 %shard_map.55 = (f32[9,64,128]{2,1,0:T(8,128)S(1)}, f32[9,64,128]{2,1,0:T(8,128)S(1)}, f32[15,64,128]{2,1,0:T(8,128)S(1)}, f32[15,64,128]{2,1,0:T(8,128)S(1)}) custom-call(s32[2]{0:T(128)S(1)} %pad_add_fusion.par, f32[24,128,128]{2,1,0:T(8,128)S(1)} %bitcast.3), custom_call_target="tpu_custom_call" | custom-call | tf_op jit(solution)/shard_map/pallas_call | solution.py:246
  2.4 0.0 copy-start.1
  2.4 13.3 %collective-permute-start.4 = (f32[15,64,128]{2,1,0:T(8,128)S(1)}, f32[15,64,128]{2,1,0:T(8,128)S(1)}, u32[]{:S(2)}, u32[]{:S(2)}) collective-permute-start(f32[15,64,128]{2,1,0:T(8,128)S(1)} %get-tuple-element.25), channel_id=1, source_target_pairs={{1,2},{2,1},{3,4},{4,3},{5,6},{6,5},{7,8},{8,7},{9,10},{10,9},{11,... | collective-permute-start | bytes 1474568 | tf_op jit(solution)/shard_map/ppermute | solution.py:263
  15.6 1.9 %collective-permute-start.5 = (f32[15,64,128]{2,1,0:T(8,128)S(1)}, f32[15,64,128]{2,1,0:T(8,128)S(1)}, u32[]{:S(2)}, u32[]{:S(2)}) collective-permute-start(f32[15,64,128]{2,1,0:T(8,128)S(1)} %get-tuple-element.26), channel_id=1, source_target_pairs={{0,1},{1,0},{2,3},{3,2},{4,5},{5,4},{6,7},{7,6},{8,9},{9,8},{10,11... | collective-permute-start | bytes 1474568 | tf_op jit(solution)/shard_map/ppermute | solution.py:263
  17.6 1.9 %collective-permute-start = (f32[9,64,128]{2,1,0:T(8,128)S(1)}, f32[9,64,128]{2,1,0:T(8,128)S(1)}, u32[]{:S(2)}, u32[]{:S(2)}) collective-permute-start(f32[9,64,128]{2,1,0:T(8,128)S(1)} %get-tuple-element.19), channel_id=1, source_target_pairs={{32,64},{64,32},{96,128},{128,96},{160,192},{192,160},{224,256},{2... | collective-permute-start | bytes 884744 | tf_op jit(solution)/shard_map/ppermute | solution.py:263
  19.5 4.8 %collective-permute-start.1 = (f32[9,64,128]{2,1,0:T(8,128)S(1)}, f32[9,64,128]{2,1,0:T(8,128)S(1)}, u32[]{:S(2)}, u32[]{:S(2)}) collective-permute-start(f32[9,64,128]{2,1,0:T(8,128)S(1)} %get-tuple-element.20), channel_id=1, source_target_pairs={{0,32},{32,0},{64,96},{96,64},{128,160},{160,128},{192,224},{224,1... | collective-permute-start | bytes 884744 | tf_op jit(solution)/shard_map/ppermute | solution.py:263
  24.3 2.5 %collective-permute-done.4.ro = f32[15,64,128]{2,1,0:T(8,128)S(1)} collective-permute-done((f32[15,64,128]{2,1,0:T(8,128)S(1)}, f32[15,64,128]{2,1,0:T(8,128)S(1)}, u32[]{:S(2)}, u32[]{:S(2)}) %collective-permute-start.4) | collective-permute-done | bytes 491552 | tf_op jit(solution)/shard_map/ppermute | solution.py:263
  26.9 3.4 %collective-permute-done.5.re = f32[15,64,128]{2,1,0:T(8,128)S(1)} collective-permute-done((f32[15,64,128]{2,1,0:T(8,128)S(1)}, f32[15,64,128]{2,1,0:T(8,128)S(1)}, u32[]{:S(2)}, u32[]{:S(2)}) %collective-permute-start.5) | collective-permute-done | bytes 491552 | tf_op jit(solution)/shard_map/ppermute | solution.py:263
  30.2 1.9 %shard_map.58 = (f32[15,128,128]{2,1,0:T(8,128)S(1)}, f32[15,64,128]{2,1,0:T(8,128)S(1)}, f32[15,64,128]{2,1,0:T(8,128)S(1)}) custom-call(s32[2]{0:T(128)S(1)} %pad_add_fusion.par, bf16[256,384]{1,0:T(8,128)(2,1)S(1)} %copy-done.2, f32[24,128,128]{2,1,0:T(8,128)S(1)} %bitcast.4, f32[15,64,128]{2,1,0:T(8,128)S(1)} %collective-permute-done.4.ro, ...), custom_call_target="tpu_custom_call" | custom-call | tf_op jit(solution)/shard_map/pallas_call | solution.py:246
  32.1 1.9 %collective-permute-start.6 = (f32[15,64,128]{2,1,0:T(8,128)S(1)}, f32[15,64,128]{2,1,0:T(8,128)S(1)}, u32[]{:S(2)}, u32[]{:S(2)}) collective-permute-start(f32[15,64,128]{2,1,0:T(8,128)S(1)} %get-tuple-element.28), channel_id=1, source_target_pairs={{32,64},{64,32},{96,128},{128,96},{160,192},{192,160},{224,256},{2... | collective-permute-start | bytes 1474568 | tf_op jit(solution)/shard_map/ppermute | solution.py:263
  34.0 4.8 %collective-permute-start.7 = (f32[15,64,128]{2,1,0:T(8,128)S(1)}, f32[15,64,128]{2,1,0:T(8,128)S(1)}, u32[]{:S(2)}, u32[]{:S(2)}) collective-permute-start(f32[15,64,128]{2,1,0:T(8,128)S(1)} %get-tuple-element.29), channel_id=1, source_target_pairs={{0,32},{32,0},{64,96},{96,64},{128,160},{160,128},{192,224},{224,1... | collective-permute-start | bytes 1474568 | tf_op jit(solution)/shard_map/ppermute | solution.py:263
  38.9 0.0 collective-permute-done.1.re
  38.9 1.3 %shard_map.56 = (f32[9,128,128]{2,1,0:T(8,128)S(1)}, f32[9,64,128]{2,1,0:T(8,128)S(1)}, f32[9,64,128]{2,1,0:T(8,128)S(1)}) custom-call(s32[2]{0:T(128)S(1)} %pad_add_fusion.par, bf16[384,256]{1,0:T(8,128)(2,1)S(1)} %copy-done.1, f32[24,128,128]{2,1,0:T(8,128)S(1)} %bitcast.5, f32[9,64,128]{2,1,0:T(8,128)S(1)} %collective-permute-done.ro, ...), custom_call_target="tpu_custom_call" | custom-call | tf_op jit(solution)/shard_map/pallas_call | solution.py:246
  40.2 3.6 %collective-permute-start.2 = (f32[9,64,128]{2,1,0:T(8,128)S(1)}, f32[9,64,128]{2,1,0:T(8,128)S(1)}, u32[]{:S(2)}, u32[]{:S(2)}) collective-permute-start(f32[9,64,128]{2,1,0:T(8,128)S(1)} %get-tuple-element.22), channel_id=1, source_target_pairs={{1,2},{2,1},{3,4},{4,3},{5,6},{6,5},{7,8},{8,7},{9,10},{10,9},{11,... | collective-permute-start | bytes 884744 | tf_op jit(solution)/shard_map/ppermute | solution.py:263
  43.8 1.9 %collective-permute-start.3 = (f32[9,64,128]{2,1,0:T(8,128)S(1)}, f32[9,64,128]{2,1,0:T(8,128)S(1)}, u32[]{:S(2)}, u32[]{:S(2)}) collective-permute-start(f32[9,64,128]{2,1,0:T(8,128)S(1)} %get-tuple-element.23), channel_id=1, source_target_pairs={{0,1},{1,0},{2,3},{3,2},{4,5},{5,4},{6,7},{7,6},{8,9},{9,8},{10,11... | collective-permute-start | bytes 884744 | tf_op jit(solution)/shard_map/ppermute | solution.py:263
  45.7 8.6 %collective-permute-done.2.ro = f32[9,64,128]{2,1,0:T(8,128)S(1)} collective-permute-done((f32[9,64,128]{2,1,0:T(8,128)S(1)}, f32[9,64,128]{2,1,0:T(8,128)S(1)}, u32[]{:S(2)}, u32[]{:S(2)}) %collective-permute-start.2) | collective-permute-done | bytes 294944 | tf_op jit(solution)/shard_map/ppermute | solution.py:263
  54.4 1.6 %shard_map.57 = (f32[9,128,128]{2,1,0:T(8,128)S(1)}, f32[128,128]{1,0:T(8,128)S(1)}) custom-call(s32[2]{0:T(128)S(1)} %pad_add_fusion.par, bf16[256,384]{1,0:T(8,128)(2,1)S(1)} %copy-done.2, f32[9,128,128]{2,1,0:T(8,128)S(1)} %get-tuple-element.21.x, f32[9,64,128]{2,1,0:T(8,128)S(1)} %collective-permute-done.2.ro, f32[9,64,128]{2,1,0:T(8,128)S(1)} %collective-permute-done.3.re), custom_call_target="tpu_custom_call" | custom-call | tf_op jit(solution)/shard_map/pallas_call | solution.py:246
  56.0 0.0 copy-start.4
  56.0 1.9 %shard_map.59 = (f32[15,128,128]{2,1,0:T(8,128)S(1)}, f32[8,48,128]{2,1,0:T(8,128)S(1)}) custom-call(s32[2]{0:T(128)S(1)} %pad_add_fusion.par, bf16[384,256]{1,0:T(8,128)(2,1)S(1)} %copy-done.1, f32[15,128,128]{2,1,0:T(8,128)S(1)} %get-tuple-element.27.x, f32[15,64,128]{2,1,0:T(8,128)S(1)} %collective-permute-done.6.ro, ...), custom_call_target="tpu_custom_call" | custom-call | tf_op jit(solution)/shard_map/pallas_call | solution.py:246
  57.9 12.5 %all_to_all.10.st = f32[8,48,128]{2,1,0:T(8,128)S(1)} all-to-all(f32[8,48,128]{2,1,0:T(8,128)S(1)} %get-tuple-element.32), channel_id=1, replica_groups={{0,1,2,3,4,5,6,7},{8,9,10,11,12,13,14,15},{16,17,18,19,20,21,22,23},{24..., dimensions={0} | all-to-all | bytes 393216 | tf_op jit(solution)/shard_map/all_to_all | solution.py:292
  70.4 9.5 %all_to_all.11.st = f32[4,48,128]{2,1,0:T(8,128)S(1)} all-to-all(f32[4,48,128]{2,1,0:T(8,128)S(1)} %shard_map.60), channel_id=1, replica_groups={{0,8,16,24},{1,9,17,25},{2,10,18,26},{3,11,19,27},{4,12,20,28},{5,13,21..., dimensions={0} | all-to-all | bytes 196608 | tf_op jit(solution)/shard_map/all_to_all | solution.py:294
  79.9 2.4 %shard_map.61 = f32[8,3,128,128]{3,2,1,0:T(8,128)} custom-call(f32[9,128,128]{2,1,0:T(8,128)S(1)} %get-tuple-element.24.fb, f32[15,128,128]{2,1,0:T(8,128)S(1)} %get-tuple-element.31.fa, f32[4,48,128]{2,1,0:T(8,128)S(1)} %all_to_all.11.st, f32[6,128]{1,0:T(8,128)S(1)} %copy-done.3, f32[128]{0:T(128)S(1)} %copy-done.4), custom_call_target="tpu_custom_call" | custom-call | tf_op jit(solution)/shard_map/pallas_call | solution.py:246
  (12 shorter events, 0.1 us)
Async XLA Ops:
  0.1 1.4 %copy-start = (f32[8,3,128,128]{3,2,1,0:T(8,128)S(1)}, f32[8,3,128,128]{3,2,1,0:T(8,128)}, u32[]{:S(2)}) copy-start(f32[8,3,128,128]{3,2,1,0:T(8,128)} %param.5) | copy-start | bytes 4718596
  1.5 28.7 %copy-start.2 = (bf16[256,384]{1,0:T(8,128)(2,1)S(1)}, bf16[256,384]{1,0:T(8,128)(2,1)}, u32[]{:S(2)}) copy-start(bf16[256,384]{1,0:T(8,128)(2,1)} %constant.30.clone.b) | copy-start | bytes 589828
  2.4 36.5 %copy-start.1 = (bf16[384,256]{1,0:T(8,128)(2,1)S(1)}, bf16[384,256]{1,0:T(8,128)(2,1)}, u32[]{:S(2)}) copy-start(bf16[384,256]{1,0:T(8,128)(2,1)} %constant.31.clone.bt) | copy-start | bytes 589828
  2.4 24.5 %collective-permute-start.4 = (f32[15,64,128]{2,1,0:T(8,128)S(1)}, f32[15,64,128]{2,1,0:T(8,128)S(1)}, u32[]{:S(2)}, u32[]{:S(2)}) collective-permute-start(f32[15,64,128]{2,1,0:T(8,128)S(1)} %get-tuple-element.25), channel_id=1, source_target_pairs={{1,2},{2,1},{3,4},{4,3},{5,6},{6,5},{7,8},{8,7},{9,10},{10,9},{11,... | collective-permute-start | bytes 1474568 | tf_op jit(solution)/shard_map/ppermute | solution.py:263
  15.6 14.6 %collective-permute-start.5 = (f32[15,64,128]{2,1,0:T(8,128)S(1)}, f32[15,64,128]{2,1,0:T(8,128)S(1)}, u32[]{:S(2)}, u32[]{:S(2)}) collective-permute-start(f32[15,64,128]{2,1,0:T(8,128)S(1)} %get-tuple-element.26), channel_id=1, source_target_pairs={{0,1},{1,0},{2,3},{3,2},{4,5},{5,4},{6,7},{7,6},{8,9},{9,8},{10,11... | collective-permute-start | bytes 1474568 | tf_op jit(solution)/shard_map/ppermute | solution.py:263
  17.6 21.3 %collective-permute-start = (f32[9,64,128]{2,1,0:T(8,128)S(1)}, f32[9,64,128]{2,1,0:T(8,128)S(1)}, u32[]{:S(2)}, u32[]{:S(2)}) collective-permute-start(f32[9,64,128]{2,1,0:T(8,128)S(1)} %get-tuple-element.19), channel_id=1, source_target_pairs={{32,64},{64,32},{96,128},{128,96},{160,192},{192,160},{224,256},{2... | collective-permute-start | bytes 884744 | tf_op jit(solution)/shard_map/ppermute | solution.py:263
  19.5 19.4 %collective-permute-start.1 = (f32[9,64,128]{2,1,0:T(8,128)S(1)}, f32[9,64,128]{2,1,0:T(8,128)S(1)}, u32[]{:S(2)}, u32[]{:S(2)}) collective-permute-start(f32[9,64,128]{2,1,0:T(8,128)S(1)} %get-tuple-element.20), channel_id=1, source_target_pairs={{0,32},{32,0},{64,96},{96,64},{128,160},{160,128},{192,224},{224,1... | collective-permute-start | bytes 884744 | tf_op jit(solution)/shard_map/ppermute | solution.py:263
  32.1 23.9 %collective-permute-start.6 = (f32[15,64,128]{2,1,0:T(8,128)S(1)}, f32[15,64,128]{2,1,0:T(8,128)S(1)}, u32[]{:S(2)}, u32[]{:S(2)}) collective-permute-start(f32[15,64,128]{2,1,0:T(8,128)S(1)} %get-tuple-element.28), channel_id=1, source_target_pairs={{32,64},{64,32},{96,128},{128,96},{160,192},{192,160},{224,256},{2... | collective-permute-start | bytes 1474568 | tf_op jit(solution)/shard_map/ppermute | solution.py:263
  34.0 22.0 %collective-permute-start.7 = (f32[15,64,128]{2,1,0:T(8,128)S(1)}, f32[15,64,128]{2,1,0:T(8,128)S(1)}, u32[]{:S(2)}, u32[]{:S(2)}) collective-permute-start(f32[15,64,128]{2,1,0:T(8,128)S(1)} %get-tuple-element.29), channel_id=1, source_target_pairs={{0,32},{32,0},{64,96},{96,64},{128,160},{160,128},{192,224},{224,1... | collective-permute-start | bytes 1474568 | tf_op jit(solution)/shard_map/ppermute | solution.py:263
  40.2 14.1 %collective-permute-start.2 = (f32[9,64,128]{2,1,0:T(8,128)S(1)}, f32[9,64,128]{2,1,0:T(8,128)S(1)}, u32[]{:S(2)}, u32[]{:S(2)}) collective-permute-start(f32[9,64,128]{2,1,0:T(8,128)S(1)} %get-tuple-element.22), channel_id=1, source_target_pairs={{1,2},{2,1},{3,4},{4,3},{5,6},{6,5},{7,8},{8,7},{9,10},{10,9},{11,... | collective-permute-start | bytes 884744 | tf_op jit(solution)/shard_map/ppermute | solution.py:263
  43.8 10.6 %collective-permute-start.3 = (f32[9,64,128]{2,1,0:T(8,128)S(1)}, f32[9,64,128]{2,1,0:T(8,128)S(1)}, u32[]{:S(2)}, u32[]{:S(2)}) collective-permute-start(f32[9,64,128]{2,1,0:T(8,128)S(1)} %get-tuple-element.23), channel_id=1, source_target_pairs={{0,1},{1,0},{2,3},{3,2},{4,5},{5,4},{6,7},{7,6},{8,9},{9,8},{10,11... | collective-permute-start | bytes 884744 | tf_op jit(solution)/shard_map/ppermute | solution.py:263
  56.0 23.9 %copy-start.3 = (f32[6,128]{1,0:T(8,128)S(1)}, f32[6,128]{1,0:T(8,128)}, u32[]{:S(2)}) copy-start(f32[6,128]{1,0:T(8,128)} %stress.1) | copy-start | bytes 9220
  56.0 23.9 %copy-start.4 = (f32[128]{0:T(128)S(1)}, f32[128]{0:T(128)}, u32[]{:S(2)}) copy-start(f32[128]{0:T(128)} %profile.1) | copy-start | bytes 1540

commit v3 on v2

--- a/solution.py
+++ b/solution.py
@@ -1,3 +1,5 @@
+import functools
+
 import jax
 import jax.numpy as jnp
 import numpy as np
@@ -10,8 +12,9 @@
 H = 64
 T = 128
 EPS = 1e-06
-NB = 9
+NB = 15
 NA = 24 - NB
+CHUNKS = [range(i, i + 6) for i in range(0, 24, 6)]
 F32 = jnp.float32
 BF = jnp.bfloat16
 
@@ -104,17 +107,26 @@
     return [range(i, min(i + step, n)) for i in range(0, n, step)]
 
 
-def pack_kernel(par, x, yo, ye, zo, ze):
+def pack_kernel(par, src, x, yo, ye, zo, ze, sems):
     off = pl.multiple_of(par[1] * H, H)
     opp = pl.multiple_of(H - off, H)
     zeven = par[0] == 0
-    for p in range(NB):
-        yo[p] = x[p, pl.ds(off, H)]
-        ye[p] = x[p, pl.ds(opp, H)]
-    for p in range(NA):
-        e, o = edges(x[NB + p], zeven)
-        ze[p] = e
-        zo[p] = o
+    copies = [
+        pltpu.make_async_copy(src.at[pl.ds(c[0], len(c))], x.at[pl.ds(c[0], len(c))], sems.at[i])
+        for i, c in enumerate(CHUNKS)
+    ]
+    for copy in copies:
+        copy.start()
+    for copy, c in zip(copies, CHUNKS):
+        copy.wait()
+        for p in c:
+            if p < NB:
+                yo[p] = x[p, pl.ds(off, H)]
+                ye[p] = x[p, pl.ds(opp, H)]
+            else:
+                e, o = edges(x[p], zeven)
+                ze[p - NB] = e
+                zo[p - NB] = o
 
 
 def y_first_kernel(par, bt, x, ro, re, n, zo, ze):
@@ -150,28 +162,22 @@
     return jnp.where(lane == p + 24, second, acc)
 
 
-def z_last_kernel(par, b, x, ro, re, f, st):
-    zeven = par[0] == 0
-    acc = jnp.zeros((T, T), F32)
-    for c in cuts(NB, 3):
-        got = z_pass(b[...], [x[p] for p in c], [re[p] for p in c], [ro[p] for p in c], zeven)
+def last(one_pass, step, flag, base, first, *refs):
+    par, b, x, ro, re = refs[:5]
+    f, st = refs[-2:]
+    even = par[flag] == 0
+    acc = jnp.zeros((T, T), F32) if first else refs[5][...]
+    for c in cuts(f.shape[0], step):
+        got = one_pass(b[...], [x[p] for p in c], [re[p] for p in c], [ro[p] for p in c], even)
         for p, v in zip(c, got):
             f[p] = v
-            acc = put_stats(acc, v, p)
-    st[...] = acc
-
-
-def y_last_kernel(par, bt, x, ro, re, acc_b, f, st):
-    yeven = par[1] == 0
-    acc = acc_b[...]
-    for c in cuts(NA, 2):
-        got = y_pass(bt[...], [x[p] for p in c], [re[p] for p in c], [ro[p] for p in c], yeven)
-        for p, v in zip(c, got):
-            f[p] = v
-            acc = put_stats(acc, v, p + NB)
-    flat = acc.T[:48]
-    for q in range(st.shape[0]):
-        st[q] = flat
+            acc = put_stats(acc, v, base + p)
+    if first:
+        st[...] = acc
+    else:
+        flat = acc.T[:48]
+        for q in range(st.shape[0]):
+            st[q] = flat
 
 
 def merge(st, tiles):
@@ -226,12 +232,15 @@
         copy.wait()
 
 
-def call(kernel, ins, outs, scratch=(), hbm_out=False):
+def call(kernel, ins, outs, scratch=(), hbm_out=False, hbm_in=()):
     smem = pl.BlockSpec(memory_space=pltpu.SMEM)
     vmem = pl.BlockSpec(memory_space=pltpu.VMEM)
     args, specs = [], []
-    for a in ins:
-        if a.dtype == jnp.int32:
+    for i, a in enumerate(ins):
+        if i in hbm_in:
+            args.append(pltpu.with_memory_space_constraint(a, pltpu.HBM))
+            specs.append(pl.BlockSpec(memory_space=pl.ANY))
+        elif a.dtype == jnp.int32:
             args.append(a)
             specs.append(smem)
         else:
@@ -275,7 +284,13 @@
     b, bt = (jnp.asarray(v) for v in bands())
     hb, ha = (NB, H, T), (NA, H, T)
     fb, fa = (NB, T, T), (NA, T, T)
-    yo, ye, zo, ze = call(pack_kernel, [par, x], [hb, hb, ha, ha])
+    x, yo, ye, zo, ze = call(
+        pack_kernel,
+        [par, x],
+        [(24, T, T), hb, hb, ha, ha],
+        scratch=[pltpu.SemaphoreType.DMA((len(CHUNKS),))],
+        hbm_in=(1,),
+    )
     yo = swap(yo, "wn", 1, False)
     ye = swap(ye, "wn", 0, False)
     zo = swap(zo, "sp", 1, True)
@@ -286,9 +301,15 @@
     n_a, yo_a, ye_a = call(z_first_kernel, [par, b, x, zo, ze], [fa, ha, ha])
     yo_a = swap(yo_a, "wn", 1, False)
     ye_a = swap(ye_a, "wn", 0, False)
-    f_b, s_b = call(z_last_kernel, [par, b, n_b, zo_b, ze_b], [fb, (T, T)])
+    f_a, s_a = call(
+        functools.partial(last, y_pass, 2, 1, NB, True), [par, bt, n_a, yo_a, ye_a], [fa, (T, T)]
+    )
+    f_b, st = call(
+        functools.partial(last, z_pass, 3, 0, 0, False),
+        [par, b, n_b, zo_b, ze_b, s_a],
+        [fb, (8, 48, T)],
+    )
     zs, xs = groups(4, 8)
-    f_a, st = call(y_last_kernel, [par, bt, n_a, yo_a, ye_a, s_b], [fa, (8, 48, T)])
     st = lax.all_to_all(st, "sp", 0, 0, axis_index_groups=zs, tiled=True)
     (st,) = call(mid_kernel, [st], [(4, 48, T)])
     st = lax.all_to_all(st, "sp", 0, 0, axis_index_groups=xs, tiled=True)

time: 82.7 us -> 72.2 us (0.87)
  waiting for transfers between devices: 14.6 us -> 4.69 us
  starting transfers between devices: 34.1 us -> 32.4 us
  Pallas kernels: 9.95 us -> 11.4 us
  local copies, waits for them, and re-layouts: 1.43 us -> 0.02 us
  blocking collectives: 22 us -> 23.1 us
    ppermute x8, waiting for transfers between devices: 14.6 us -> 4.69 us  [swap(): return lax.ppermute(v, axis, pairs)]
    ppermute x8, starting transfers between devices: 34.1 us -> 32.4 us  [swap(): return lax.ppermute(v, axis, pairs)]
    pallas_call x7, Pallas kernels: 9.95 us -> 11.4 us  [call(): pl.pallas_call(kernel, in_specs=specs, out_specs=out_specs, out_shape=sha...]
    unnamed x10 -> x8, local copies, waits for them, and re-layouts: 1.43 us -> 0.02 us
    all_to_all x1, blocking collectives: 12.5 us -> 13.5 us  [run(): st = lax.all_to_all(st, 'sp', 0, 0, axis_index_groups=zs, tiled=True)]
where the time goes in v3:
time: 72.2 us; the launch traced here: 71.8 us
  starting transfers between devices  32.4 us (45%)
  blocking collectives  23.1 us (32%)
  Pallas kernels  11.4 us (16%)
  waiting for transfers between devices  4.69 us (6%)
    ppermute x8, starting transfers between devices, swap(): return lax.ppermute(v, axis, pairs)  32.4 us
    all_to_all x1, blocking collectives, run(): st = lax.all_to_all(st, 'sp', 0, 0, axis_index_groups=zs, tiled=True)  13.5 us
    pallas_call x7, Pallas kernels, call(): pl.pallas_call(kernel, in_specs=specs, out_specs=out_specs, out_shape=sha...  11.4 us
    all_to_all x1, blocking collectives, run(): st = lax.all_to_all(st, 'sp', 0, 0, axis_index_groups=xs, tiled=True)  9.58 us
    ppermute x8, waiting for transfers between devices, swap(): return lax.ppermute(v, axis, pairs)  4.69 us
  transfers between devices with their start and end apart: 8, of which 3 were waited for; matrix products, arithmetic and copies ran while one was open for 0% of the time, Pallas kernels for 6%

profile of v3, /device:TPU:24, one launch (start us, length us, event | category | flops | bytes accessed | tf_op | source)
XLA Modules:
  0.0 71.8 jit_solution(17630410731045747763)
XLA Ops:
  0.0 0.1 pad_add_fusion.par.refs_0_
  0.1 2.1 %shard_map.55 = (f32[24,128,128]{2,1,0:T(8,128)S(1)}, f32[15,64,128]{2,1,0:T(8,128)S(1)}, f32[15,64,128]{2,1,0:T(8,128)S(1)}, f32[9,64,128]{2,1,0:T(8,128)S(1)}, f32[9,64,128]{2,1,0:T(8,128)S(1)}) custom-call(s32[2]{0:T(128)S(1)} %pad_add_fusion.par.refs_0_, f32[24,128,128]{2,1,0:T(8,128)} %bitcast.3), custom_call_target="tpu_custom_call" | custom-call | tf_op jit(solution)/shard_map/pallas_call | solution.py:255
  2.2 0.0 copy-start
  2.2 2.1 %collective-permute-start = (f32[15,64,128]{2,1,0:T(8,128)S(1)}, f32[15,64,128]{2,1,0:T(8,128)S(1)}, u32[]{:S(2)}, u32[]{:S(2)}) collective-permute-start(f32[15,64,128]{2,1,0:T(8,128)S(1)} %get-tuple-element.21), channel_id=1, source_target_pairs={{32,64},{64,32},{96,128},{128,96},{160,192},{192,160},{224,256},{2... | collective-permute-start | bytes 1474568 | tf_op jit(solution)/shard_map/ppermute | solution.py:272
  4.3 4.8 %collective-permute-start.1 = (f32[15,64,128]{2,1,0:T(8,128)S(1)}, f32[15,64,128]{2,1,0:T(8,128)S(1)}, u32[]{:S(2)}, u32[]{:S(2)}) collective-permute-start(f32[15,64,128]{2,1,0:T(8,128)S(1)} %get-tuple-element.22), channel_id=1, source_target_pairs={{0,32},{32,0},{64,96},{96,64},{128,160},{160,128},{192,224},{224,1... | collective-permute-start | bytes 1474568 | tf_op jit(solution)/shard_map/ppermute | solution.py:272
  9.1 13.1 %collective-permute-start.4 = (f32[9,64,128]{2,1,0:T(8,128)S(1)}, f32[9,64,128]{2,1,0:T(8,128)S(1)}, u32[]{:S(2)}, u32[]{:S(2)}) collective-permute-start(f32[9,64,128]{2,1,0:T(8,128)S(1)} %get-tuple-element.26), channel_id=1, source_target_pairs={{1,2},{2,1},{3,4},{4,3},{5,6},{6,5},{7,8},{8,7},{9,10},{10,9},{11,... | collective-permute-start | bytes 884744 | tf_op jit(solution)/shard_map/ppermute | solution.py:272
  22.2 1.9 %collective-permute-start.5 = (f32[9,64,128]{2,1,0:T(8,128)S(1)}, f32[9,64,128]{2,1,0:T(8,128)S(1)}, u32[]{:S(2)}, u32[]{:S(2)}) collective-permute-start(f32[9,64,128]{2,1,0:T(8,128)S(1)} %get-tuple-element.27), channel_id=1, source_target_pairs={{0,1},{1,0},{2,3},{3,2},{4,5},{5,4},{6,7},{7,6},{8,9},{9,8},{10,11... | collective-permute-start | bytes 884744 | tf_op jit(solution)/shard_map/ppermute | solution.py:272
  24.2 1.7 %shard_map.56 = (f32[15,128,128]{2,1,0:T(8,128)S(1)}, f32[15,64,128]{2,1,0:T(8,128)S(1)}, f32[15,64,128]{2,1,0:T(8,128)S(1)}) custom-call(s32[2]{0:T(128)S(1)} %pad_add_fusion.par.refs_0_, bf16[384,256]{1,0:T(8,128)(2,1)S(1)} %copy-done.1, f32[24,128,128]{2,1,0:T(8,128)S(1)} %get-tuple-element.20.x, f32[15,64,128]{2,1,0:T(8,128)S(1)} %collective-permute-done.ro, ...), custom_call_target="tpu_custom_call" | custom-call | tf_op jit(solution)/shard_map/pallas_call | solution.py:255
  25.9 3.0 %collective-permute-start.2 = (f32[15,64,128]{2,1,0:T(8,128)S(1)}, f32[15,64,128]{2,1,0:T(8,128)S(1)}, u32[]{:S(2)}, u32[]{:S(2)}) collective-permute-start(f32[15,64,128]{2,1,0:T(8,128)S(1)} %get-tuple-element.24), channel_id=1, source_target_pairs={{1,2},{2,1},{3,4},{4,3},{5,6},{6,5},{7,8},{8,7},{9,10},{10,9},{11,... | collective-permute-start | bytes 1474568 | tf_op jit(solution)/shard_map/ppermute | solution.py:272
  28.9 2.8 %collective-permute-start.3 = (f32[15,64,128]{2,1,0:T(8,128)S(1)}, f32[15,64,128]{2,1,0:T(8,128)S(1)}, u32[]{:S(2)}, u32[]{:S(2)}) collective-permute-start(f32[15,64,128]{2,1,0:T(8,128)S(1)} %get-tuple-element.25), channel_id=1, source_target_pairs={{0,1},{1,0},{2,3},{3,2},{4,5},{5,4},{6,7},{7,6},{8,9},{9,8},{10,11... | collective-permute-start | bytes 1474568 | tf_op jit(solution)/shard_map/ppermute | solution.py:272
  31.8 1.0 %collective-permute-done.5.re = f32[9,64,128]{2,1,0:T(8,128)S(1)} collective-permute-done((f32[9,64,128]{2,1,0:T(8,128)S(1)}, f32[9,64,128]{2,1,0:T(8,128)S(1)}, u32[]{:S(2)}, u32[]{:S(2)}) %collective-permute-start.5) | collective-permute-done | bytes 294944 | tf_op jit(solution)/shard_map/ppermute | solution.py:272
  32.8 1.4 %shard_map.57 = (f32[9,128,128]{2,1,0:T(8,128)S(1)}, f32[9,64,128]{2,1,0:T(8,128)S(1)}, f32[9,64,128]{2,1,0:T(8,128)S(1)}) custom-call(s32[2]{0:T(128)S(1)} %pad_add_fusion.par.refs_0_, bf16[256,384]{1,0:T(8,128)(2,1)S(1)} %copy-done, f32[24,128,128]{2,1,0:T(8,128)S(1)} %get-tuple-element.20.x, f32[9,64,128]{2,1,0:T(8,128)S(1)} %collective-permute-done.4.ro, ...), custom_call_target="tpu_custom_call" | custom-call | tf_op jit(solution)/shard_map/pallas_call | solution.py:255
  34.2 1.9 %collective-permute-start.6 = (f32[9,64,128]{2,1,0:T(8,128)S(1)}, f32[9,64,128]{2,1,0:T(8,128)S(1)}, u32[]{:S(2)}, u32[]{:S(2)}) collective-permute-start(f32[9,64,128]{2,1,0:T(8,128)S(1)} %get-tuple-element.29), channel_id=1, source_target_pairs={{32,64},{64,32},{96,128},{128,96},{160,192},{192,160},{224,256},{2... | collective-permute-start | bytes 884744 | tf_op jit(solution)/shard_map/ppermute | solution.py:272
  36.1 2.7 %collective-permute-start.7 = (f32[9,64,128]{2,1,0:T(8,128)S(1)}, f32[9,64,128]{2,1,0:T(8,128)S(1)}, u32[]{:S(2)}, u32[]{:S(2)}) collective-permute-start(f32[9,64,128]{2,1,0:T(8,128)S(1)} %get-tuple-element.30), channel_id=1, source_target_pairs={{0,32},{32,0},{64,96},{96,64},{128,160},{160,128},{192,224},{224,1... | collective-permute-start | bytes 884744 | tf_op jit(solution)/shard_map/ppermute | solution.py:272
  38.8 3.4 %collective-permute-done.6.refs_3_ = f32[9,64,128]{2,1,0:T(8,128)S(1)} collective-permute-done((f32[9,64,128]{2,1,0:T(8,128)S(1)}, f32[9,64,128]{2,1,0:T(8,128)S(1)}, u32[]{:S(2)}, u32[]{:S(2)}) %collective-permute-start.6) | collective-permute-done | bytes 294944 | tf_op jit(solution)/shard_map/ppermute | solution.py:272
  42.2 0.0 collective-permute-done.7.refs_4_
  42.2 1.4 %shard_map.58 = (f32[9,128,128]{2,1,0:T(8,128)S(1)}, f32[128,128]{1,0:T(8,128)S(1)}) custom-call(s32[2]{0:T(128)S(1)} %pad_add_fusion.par.refs_0_, bf16[384,256]{1,0:T(8,128)(2,1)S(1)} %copy-done.1, f32[9,128,128]{2,1,0:T(8,128)S(1)} %get-tuple-element.28.refs_2_, f32[9,64,128]{2,1,0:T(8,128)S(1)} %collective-permute-done.6.refs_3_, ...), custom_call_target="tpu_custom_call" | custom-call | tf_op jit(solution)/shard_map/pallas_call | solution.py:255
  43.7 0.0 copy-start.2
  43.7 0.0 copy-start.3
  43.7 0.3 collective-permute-done.2.refs_3_
  44.0 2.3 %shard_map.59 = (f32[15,128,128]{2,1,0:T(8,128)S(1)}, f32[8,48,128]{2,1,0:T(8,128)S(1)}) custom-call(s32[2]{0:T(128)S(1)} %pad_add_fusion.par.refs_0_, bf16[256,384]{1,0:T(8,128)(2,1)S(1)} %copy-done, f32[15,128,128]{2,1,0:T(8,128)S(1)} %get-tuple-element.23.refs_2_, f32[15,64,128]{2,1,0:T(8,128)S(1)} %collective-permute-done.2.refs_3_, ...), custom_call_target="tpu_custom_call" | custom-call | tf_op jit(solution)/shard_map/pallas_call | solution.py:255
  46.3 13.5 %all_to_all.10.st = f32[8,48,128]{2,1,0:T(8,128)S(1)} all-to-all(f32[8,48,128]{2,1,0:T(8,128)S(1)} %get-tuple-element.34), channel_id=1, replica_groups={{0,1,2,3,4,5,6,7},{8,9,10,11,12,13,14,15},{16,17,18,19,20,21,22,23},{24..., dimensions={0} | all-to-all | bytes 393216 | tf_op jit(solution)/shard_map/all_to_all | solution.py:313
  59.8 9.6 %all_to_all.11.st = f32[4,48,128]{2,1,0:T(8,128)S(1)} all-to-all(f32[4,48,128]{2,1,0:T(8,128)S(1)} %shard_map.60), channel_id=1, replica_groups={{0,8,16,24},{1,9,17,25},{2,10,18,26},{3,11,19,27},{4,12,20,28},{5,13,21..., dimensions={0} | all-to-all | bytes 196608 | tf_op jit(solution)/shard_map/all_to_all | solution.py:315
  69.4 2.4 %shard_map.61 = f32[8,3,128,128]{3,2,1,0:T(8,128)} custom-call(f32[15,128,128]{2,1,0:T(8,128)S(1)} %get-tuple-element.32.fb, f32[9,128,128]{2,1,0:T(8,128)S(1)} %get-tuple-element.33.fa, f32[4,48,128]{2,1,0:T(8,128)S(1)} %all_to_all.11.st, f32[6,128]{1,0:T(8,128)S(1)} %copy-done.2, f32[128]{0:T(128)S(1)} %copy-done.3), custom_call_target="tpu_custom_call" | custom-call | tf_op jit(solution)/shard_map/pallas_call | solution.py:255
  (10 shorter events, 0.0 us)
Async XLA Ops:
  0.0 24.2 %copy-start.1 = (bf16[384,256]{1,0:T(8,128)(2,1)S(1)}, bf16[384,256]{1,0:T(8,128)(2,1)}, u32[]{:S(2)}) copy-start(bf16[384,256]{1,0:T(8,128)(2,1)} %constant.31.clone.bt.refs_1_) | copy-start | bytes 589828
  2.2 30.6 %copy-start = (bf16[256,384]{1,0:T(8,128)(2,1)S(1)}, bf16[256,384]{1,0:T(8,128)(2,1)}, u32[]{:S(2)}) copy-start(bf16[256,384]{1,0:T(8,128)(2,1)} %constant.30.clone.b.refs_1_) | copy-start | bytes 589828
  2.2 21.9 %collective-permute-start = (f32[15,64,128]{2,1,0:T(8,128)S(1)}, f32[15,64,128]{2,1,0:T(8,128)S(1)}, u32[]{:S(2)}, u32[]{:S(2)}) collective-permute-start(f32[15,64,128]{2,1,0:T(8,128)S(1)} %get-tuple-element.21), channel_id=1, source_target_pairs={{32,64},{64,32},{96,128},{128,96},{160,192},{192,160},{224,256},{2... | collective-permute-start | bytes 1474568 | tf_op jit(solution)/shard_map/ppermute | solution.py:272
  4.3 19.9 %collective-permute-start.1 = (f32[15,64,128]{2,1,0:T(8,128)S(1)}, f32[15,64,128]{2,1,0:T(8,128)S(1)}, u32[]{:S(2)}, u32[]{:S(2)}) collective-permute-start(f32[15,64,128]{2,1,0:T(8,128)S(1)} %get-tuple-element.22), channel_id=1, source_target_pairs={{0,32},{32,0},{64,96},{96,64},{128,160},{160,128},{192,224},{224,1... | collective-permute-start | bytes 1474568 | tf_op jit(solution)/shard_map/ppermute | solution.py:272
  9.1 22.7 %collective-permute-start.4 = (f32[9,64,128]{2,1,0:T(8,128)S(1)}, f32[9,64,128]{2,1,0:T(8,128)S(1)}, u32[]{:S(2)}, u32[]{:S(2)}) collective-permute-start(f32[9,64,128]{2,1,0:T(8,128)S(1)} %get-tuple-element.26), channel_id=1, source_target_pairs={{1,2},{2,1},{3,4},{4,3},{5,6},{6,5},{7,8},{8,7},{9,10},{10,9},{11,... | collective-permute-start | bytes 884744 | tf_op jit(solution)/shard_map/ppermute | solution.py:272
  22.2 10.5 %collective-permute-start.5 = (f32[9,64,128]{2,1,0:T(8,128)S(1)}, f32[9,64,128]{2,1,0:T(8,128)S(1)}, u32[]{:S(2)}, u32[]{:S(2)}) collective-permute-start(f32[9,64,128]{2,1,0:T(8,128)S(1)} %get-tuple-element.27), channel_id=1, source_target_pairs={{0,1},{1,0},{2,3},{3,2},{4,5},{5,4},{6,7},{7,6},{8,9},{9,8},{10,11... | collective-permute-start | bytes 884744 | tf_op jit(solution)/shard_map/ppermute | solution.py:272
  25.9 18.1 %collective-permute-start.2 = (f32[15,64,128]{2,1,0:T(8,128)S(1)}, f32[15,64,128]{2,1,0:T(8,128)S(1)}, u32[]{:S(2)}, u32[]{:S(2)}) collective-permute-start(f32[15,64,128]{2,1,0:T(8,128)S(1)} %get-tuple-element.24), channel_id=1, source_target_pairs={{1,2},{2,1},{3,4},{4,3},{5,6},{6,5},{7,8},{8,7},{9,10},{10,9},{11,... | collective-permute-start | bytes 1474568 | tf_op jit(solution)/shard_map/ppermute | solution.py:272
  28.9 15.1 %collective-permute-start.3 = (f32[15,64,128]{2,1,0:T(8,128)S(1)}, f32[15,64,128]{2,1,0:T(8,128)S(1)}, u32[]{:S(2)}, u32[]{:S(2)}) collective-permute-start(f32[15,64,128]{2,1,0:T(8,128)S(1)} %get-tuple-element.25), channel_id=1, source_target_pairs={{0,1},{1,0},{2,3},{3,2},{4,5},{5,4},{6,7},{7,6},{8,9},{9,8},{10,11... | collective-permute-start | bytes 1474568 | tf_op jit(solution)/shard_map/ppermute | solution.py:272
  34.2 8.0 %collective-permute-start.6 = (f32[9,64,128]{2,1,0:T(8,128)S(1)}, f32[9,64,128]{2,1,0:T(8,128)S(1)}, u32[]{:S(2)}, u32[]{:S(2)}) collective-permute-start(f32[9,64,128]{2,1,0:T(8,128)S(1)} %get-tuple-element.29), channel_id=1, source_target_pairs={{32,64},{64,32},{96,128},{128,96},{160,192},{192,160},{224,256},{2... | collective-permute-start | bytes 884744 | tf_op jit(solution)/shard_map/ppermute | solution.py:272
  36.1 6.1 %collective-permute-start.7 = (f32[9,64,128]{2,1,0:T(8,128)S(1)}, f32[9,64,128]{2,1,0:T(8,128)S(1)}, u32[]{:S(2)}, u32[]{:S(2)}) collective-permute-start(f32[9,64,128]{2,1,0:T(8,128)S(1)} %get-tuple-element.30), channel_id=1, source_target_pairs={{0,32},{32,0},{64,96},{96,64},{128,160},{160,128},{192,224},{224,1... | collective-permute-start | bytes 884744 | tf_op jit(solution)/shard_map/ppermute | solution.py:272
  43.7 25.7 %copy-start.2 = (f32[6,128]{1,0:T(8,128)S(1)}, f32[6,128]{1,0:T(8,128)}, u32[]{:S(2)}) copy-start(f32[6,128]{1,0:T(8,128)} %stress.1) | copy-start | bytes 9220
  43.7 25.7 %copy-start.3 = (f32[128]{0:T(128)S(1)}, f32[128]{0:T(128)}, u32[]{:S(2)}) copy-start(f32[128]{0:T(128)} %profile.1) | copy-start | bytes 1540

commit v4 on v3

--- a/solution.py
+++ b/solution.py
@@ -14,7 +14,6 @@
 EPS = 1e-06
 NB = 15
 NA = 24 - NB
-CHUNKS = [range(i, i + 6) for i in range(0, 24, 6)]
 F32 = jnp.float32
 BF = jnp.bfloat16
 
@@ -42,6 +41,10 @@
     low = (b - h.astype(np.float32) - m.astype(np.float32)).astype(BF)
     across = np.concatenate([h, m, low], axis=1)
     return np.ascontiguousarray(across), np.ascontiguousarray(across.T)
+
+
+def parity(axis):
+    return lax.axis_index(axis) % 2
 
 
 def lanes_low(shape):
@@ -107,30 +110,27 @@
     return [range(i, min(i + step, n)) for i in range(0, n, step)]
 
 
-def pack_kernel(par, src, x, yo, ye, zo, ze, sems):
-    off = pl.multiple_of(par[1] * H, H)
+def pack_y_kernel(src, yo, ye, sems):
+    off = pl.multiple_of(parity("wn") * H, H)
     opp = pl.multiple_of(H - off, H)
-    zeven = par[0] == 0
-    copies = [
-        pltpu.make_async_copy(src.at[pl.ds(c[0], len(c))], x.at[pl.ds(c[0], len(c))], sems.at[i])
-        for i, c in enumerate(CHUNKS)
-    ]
-    for copy in copies:
-        copy.start()
-    for copy, c in zip(copies, CHUNKS):
-        copy.wait()
-        for p in c:
-            if p < NB:
-                yo[p] = x[p, pl.ds(off, H)]
-                ye[p] = x[p, pl.ds(opp, H)]
-            else:
-                e, o = edges(x[p], zeven)
-                ze[p - NB] = e
-                zo[p - NB] = o
-
-
-def y_first_kernel(par, bt, x, ro, re, n, zo, ze):
-    zeven, yeven = par[0] == 0, par[1] == 0
+    one = pltpu.make_async_copy(src.at[pl.ds(0, NB), pl.ds(off, H)], yo, sems.at[0])
+    two = pltpu.make_async_copy(src.at[pl.ds(0, NB), pl.ds(opp, H)], ye, sems.at[1])
+    one.start()
+    two.start()
+    one.wait()
+    two.wait()
+
+
+def pack_z_kernel(x, zo, ze):
+    zeven = parity("sp") == 0
+    for p in range(NA):
+        e, o = edges(x[NB + p], zeven)
+        ze[p] = e
+        zo[p] = o
+
+
+def y_first_kernel(bt, x, ro, re, n, zo, ze):
+    zeven, yeven = parity("sp") == 0, parity("wn") == 0
     for c in cuts(NB, 2):
         got = y_pass(bt[...], [x[p] for p in c], [re[p] for p in c], [ro[p] for p in c], yeven)
         for p, v in zip(c, got):
@@ -140,9 +140,8 @@
             zo[p] = o
 
 
-def z_first_kernel(par, b, x, ro, re, n, yo, ye):
-    off = par[1]
-    zeven, yeven = par[0] == 0, off == 0
+def z_first_kernel(b, x, ro, re, n, yo, ye):
+    zeven, yeven = parity("sp") == 0, parity("wn") == 0
     for c in cuts(NA, 3):
         got = z_pass(
             b[...], [x[NB + p] for p in c], [re[p] for p in c], [ro[p] for p in c], zeven
@@ -162,11 +161,11 @@
     return jnp.where(lane == p + 24, second, acc)
 
 
-def last(one_pass, step, flag, base, first, *refs):
-    par, b, x, ro, re = refs[:5]
+def last(one_pass, step, axis, base, first, *refs):
+    b, x, ro, re = refs[:4]
     f, st = refs[-2:]
-    even = par[flag] == 0
-    acc = jnp.zeros((T, T), F32) if first else refs[5][...]
+    even = parity(axis) == 0
+    acc = jnp.zeros((T, T), F32) if first else refs[4][...]
     for c in cuts(f.shape[0], step):
         got = one_pass(b[...], [x[p] for p in c], [re[p] for p in c], [ro[p] for p in c], even)
         for p, v in zip(c, got):
@@ -196,9 +195,7 @@
         out[q, 24:] = second
 
 
-def final_kernel(fb, fa, st, stress, profile, out, buf, sems):
-    mean, second = merge(st, 8)
-    inv = 1.0 / jnp.sqrt(second * (1.0 / 4096.0) + EPS)
+def factor_kernel(stress, profile, wide):
     s = stress[...]
     a11 = jnp.sqrt(s[0:1])
     a21 = s[3:4] / a11
@@ -206,25 +203,26 @@
     a31 = s[4:5] / a11
     a32 = (s[5:6] - a21 * a31) / a22
     a33 = jnp.sqrt(s[2:3] - a31 * a31 - a32 * a32)
-    prof = profile[...].reshape(1, T)
-    rows = []
-    for k in range(8):
-        i0, i1, i2 = (inv[3 * k + c : 3 * k + c + 1] for c in range(3))
-        rows += [a11 * i0, a21 * i0, a22 * i1, a31 * i0, a32 * i1, a33 * i2]
-    table = jnp.concatenate([mean] + rows + [prof], axis=0)
-    cols = jnp.concatenate([table, jnp.zeros((T - 73, T), F32)], axis=0).T
-    pcol = cols[:, 72:73]
+    rows = [a11, a21, a22, a31, a32, a33, profile[...].reshape(1, T), a11]
+    cols = jnp.concatenate(rows + [jnp.zeros((T - 8, T), F32)], axis=0).T
+    for q in range(7):
+        wide[q] = jnp.broadcast_to(cols[:, q : q + 1], (T, T))
+
+
+def final_kernel(fb, fa, st, wide, out, buf, sems):
+    mean, second = merge(st, 8)
+    inv = 1.0 / jnp.sqrt(second * (1.0 / 4096.0) + EPS)
+    cols = jnp.concatenate([mean, inv, jnp.zeros((T - 48, T), F32)], axis=0).T
     copies = []
     for k in range(8):
         g = []
         for c in range(3):
             p = 3 * k + c
             v = fb[p] if p < NB else fa[p - NB]
-            g.append(v - cols[:, p : p + 1])
-        w = [cols[:, 24 + 6 * k + q : 25 + 6 * k + q] for q in range(6)]
-        buf[k, 0] = pcol + w[0] * g[0]
-        buf[k, 1] = w[1] * g[0] + w[2] * g[1]
-        buf[k, 2] = w[3] * g[0] + w[4] * g[1] + w[5] * g[2]
+            g.append((v - cols[:, p : p + 1]) * cols[:, 24 + p : 25 + p])
+        buf[k, 0] = wide[6] + wide[0] * g[0]
+        buf[k, 1] = wide[1] * g[0] + wide[2] * g[1]
+        buf[k, 2] = wide[3] * g[0] + wide[4] * g[1] + wide[5] * g[2]
         copy = pltpu.make_async_copy(buf.at[k], out.at[k], sems.at[k])
         copy.start()
         copies.append(copy)
@@ -233,16 +231,12 @@
 
 
 def call(kernel, ins, outs, scratch=(), hbm_out=False, hbm_in=()):
-    smem = pl.BlockSpec(memory_space=pltpu.SMEM)
     vmem = pl.BlockSpec(memory_space=pltpu.VMEM)
     args, specs = [], []
     for i, a in enumerate(ins):
         if i in hbm_in:
             args.append(pltpu.with_memory_space_constraint(a, pltpu.HBM))
             specs.append(pl.BlockSpec(memory_space=pl.ANY))
-        elif a.dtype == jnp.int32:
-            args.append(a)
-            specs.append(smem)
         else:
             args.append(pltpu.with_memory_space_constraint(a, pltpu.VMEM))
             specs.append(vmem)
@@ -280,33 +274,36 @@
 
 def run(random_slabs, stress, profile):
     x = random_slabs.reshape(24, T, T)
-    par = jnp.stack([lax.axis_index("sp") % 2, lax.axis_index("wn") % 2]).astype(jnp.int32)
     b, bt = (jnp.asarray(v) for v in bands())
     hb, ha = (NB, H, T), (NA, H, T)
     fb, fa = (NB, T, T), (NA, T, T)
-    x, yo, ye, zo, ze = call(
-        pack_kernel,
-        [par, x],
-        [(24, T, T), hb, hb, ha, ha],
-        scratch=[pltpu.SemaphoreType.DMA((len(CHUNKS),))],
-        hbm_in=(1,),
+    yo, ye = call(
+        pack_y_kernel,
+        [x],
+        [hb, hb],
+        scratch=[pltpu.SemaphoreType.DMA((2,))],
+        hbm_in=(0,),
     )
     yo = swap(yo, "wn", 1, False)
+    zo, ze = call(pack_z_kernel, [x], [ha, ha])
+    zo = swap(zo, "sp", 1, True)
     ye = swap(ye, "wn", 0, False)
-    zo = swap(zo, "sp", 1, True)
     ze = swap(ze, "sp", 0, True)
-    n_b, zo_b, ze_b = call(y_first_kernel, [par, bt, x, yo, ye], [fb, hb, hb])
+    n_b, zo_b, ze_b = call(y_first_kernel, [bt, x, yo, ye], [fb, hb, hb])
     zo_b = swap(zo_b, "sp", 1, True)
     ze_b = swap(ze_b, "sp", 0, True)
-    n_a, yo_a, ye_a = call(z_first_kernel, [par, b, x, zo, ze], [fa, ha, ha])
+    n_a, yo_a, ye_a = call(z_first_kernel, [b, x, zo, ze], [fa, ha, ha])
     yo_a = swap(yo_a, "wn", 1, False)
     ye_a = swap(ye_a, "wn", 0, False)
+    (wide,) = call(factor_kernel, [stress, profile], [(7, T, T)])
     f_a, s_a = call(
-        functools.partial(last, y_pass, 2, 1, NB, True), [par, bt, n_a, yo_a, ye_a], [fa, (T, T)]
+        functools.partial(last, y_pass, 2, "wn", NB, True),
+        [bt, n_a, yo_a, ye_a],
+        [fa, (T, T)],
     )
     f_b, st = call(
-        functools.partial(last, z_pass, 3, 0, 0, False),
-        [par, b, n_b, zo_b, ze_b, s_a],
+        functools.partial(last, z_pass, 3, "sp", 0, False),
+        [b, n_b, zo_b, ze_b, s_a],
         [fb, (8, 48, T)],
     )
     zs, xs = groups(4, 8)
@@ -315,7 +312,7 @@
     st = lax.all_to_all(st, "sp", 0, 0, axis_index_groups=xs, tiled=True)
     (out,) = call(
         final_kernel,
-        [f_b, f_a, st, stress, profile],
+        [f_b, f_a, st, wide],
         [(8, 3, T, T)],
         scratch=[pltpu.VMEM((8, 3, T, T), F32), pltpu.SemaphoreType.DMA((8,))],
         hbm_out=True,

time: 72.2 us -> 69.6 us (0.964)
  the two profiles are of different devices: /device:TPU:24 before, /device:TPU:16 now
where the time goes in v4:
time: 69.6 us; the launch traced here: 69.1 us
  starting transfers between devices  36.6 us (53%)
  blocking collectives  14.4 us (21%)
  waiting for transfers between devices  9.08 us (13%)
  Pallas kernels  8.83 us (13%)
    ppermute x8, starting transfers between devices, swap(): return lax.ppermute(v, axis, pairs)  33.3 us
    all_to_all x1, blocking collectives, run(): st = lax.all_to_all(st, 'sp', 0, 0, axis_index_groups=zs, tiled=True)  14.4 us
    pallas_call x9, Pallas kernels, call(): pl.pallas_call(kernel, in_specs=specs, out_specs=out_specs, out_shape=sha...  8.83 us
    all_to_all x1, waiting for transfers between devices, run(): st = lax.all_to_all(st, 'sp', 0, 0, axis_index_groups=xs, tiled=True)  5.39 us
    ppermute x8, waiting for transfers between devices, swap(): return lax.ppermute(v, axis, pairs)  3.69 us
    all_to_all x1, starting transfers between devices, run(): st = lax.all_to_all(st, 'sp', 0, 0, axis_index_groups=xs, tiled=True)  3.3 us
  transfers between devices with their start and end apart: 9, of which 4 were waited for; matrix products, arithmetic and copies ran while one was open for 0% of the time, Pallas kernels for 5%

profile of v4, /device:TPU:16, one launch (start us, length us, event | category | flops | bytes accessed | tf_op | source)
XLA Modules:
  0.0 69.1 jit_solution(8995764556519199827)
XLA Ops:
  0.0 1.3 %shard_map.55 = (f32[15,64,128]{2,1,0:T(8,128)S(1)}, f32[15,64,128]{2,1,0:T(8,128)S(1)}) custom-call(f32[24,128,128]{2,1,0:T(8,128)} %bitcast.1), custom_call_target="tpu_custom_call" | custom-call | tf_op jit(solution)/shard_map/pallas_call | solution.py:249
  1.3 1.9 %collective-permute-start = (f32[15,64,128]{2,1,0:T(8,128)S(1)}, f32[15,64,128]{2,1,0:T(8,128)S(1)}, u32[]{:S(2)}, u32[]{:S(2)}) collective-permute-start(f32[15,64,128]{2,1,0:T(8,128)S(1)} %get-tuple-element.19), channel_id=1, source_target_pairs={{32,64},{64,32},{96,128},{128,96},{160,192},{192,160},{224,256},{2... | collective-permute-start | bytes 1474568 | tf_op jit(solution)/shard_map/ppermute | solution.py:266
  3.3 3.6 %collective-permute-start.1 = (f32[15,64,128]{2,1,0:T(8,128)S(1)}, f32[15,64,128]{2,1,0:T(8,128)S(1)}, u32[]{:S(2)}, u32[]{:S(2)}) collective-permute-start(f32[15,64,128]{2,1,0:T(8,128)S(1)} %get-tuple-element.20), channel_id=1, source_target_pairs={{0,32},{32,0},{64,96},{96,64},{128,160},{160,128},{192,224},{224,1... | collective-permute-start | bytes 1474568 | tf_op jit(solution)/shard_map/ppermute | solution.py:266
  6.9 0.2 shard_map.57
  7.1 0.0 copy-start.1
  7.1 13.3 %collective-permute-start.4 = (f32[9,64,128]{2,1,0:T(8,128)S(1)}, f32[9,64,128]{2,1,0:T(8,128)S(1)}, u32[]{:S(2)}, u32[]{:S(2)}) collective-permute-start(f32[9,64,128]{2,1,0:T(8,128)S(1)} %get-tuple-element.24), channel_id=1, source_target_pairs={{1,2},{2,1},{3,4},{4,3},{5,6},{6,5},{7,8},{8,7},{9,10},{10,9},{11,... | collective-permute-start | bytes 884744 | tf_op jit(solution)/shard_map/ppermute | solution.py:266
  20.4 1.9 %collective-permute-start.5 = (f32[9,64,128]{2,1,0:T(8,128)S(1)}, f32[9,64,128]{2,1,0:T(8,128)S(1)}, u32[]{:S(2)}, u32[]{:S(2)}) collective-permute-start(f32[9,64,128]{2,1,0:T(8,128)S(1)} %get-tuple-element.25), channel_id=1, source_target_pairs={{0,1},{1,0},{2,3},{3,2},{4,5},{5,4},{6,7},{7,6},{8,9},{9,8},{10,11... | collective-permute-start | bytes 884744 | tf_op jit(solution)/shard_map/ppermute | solution.py:266
  22.3 1.1 %shard_map.56 = (f32[15,128,128]{2,1,0:T(8,128)S(1)}, f32[15,64,128]{2,1,0:T(8,128)S(1)}, f32[15,64,128]{2,1,0:T(8,128)S(1)}) custom-call(bf16[384,256]{1,0:T(8,128)(2,1)S(1)} %copy-done.2, f32[24,128,128]{2,1,0:T(8,128)S(1)} %bitcast.3, f32[15,64,128]{2,1,0:T(8,128)S(1)} %collective-permute-done.ro, f32[15,64,128]{2,1,0:T(8,128)S(1)} %collective-permute-done.1.re), custom_call_target="tpu_custom_call" | custom-call | tf_op jit(solution)/shard_map/pallas_call | solution.py:249
  23.5 3.0 %collective-permute-start.2 = (f32[15,64,128]{2,1,0:T(8,128)S(1)}, f32[15,64,128]{2,1,0:T(8,128)S(1)}, u32[]{:S(2)}, u32[]{:S(2)}) collective-permute-start(f32[15,64,128]{2,1,0:T(8,128)S(1)} %get-tuple-element.22), channel_id=1, source_target_pairs={{1,2},{2,1},{3,4},{4,3},{5,6},{6,5},{7,8},{8,7},{9,10},{10,9},{11,... | collective-permute-start | bytes 1474568 | tf_op jit(solution)/shard_map/ppermute | solution.py:266
  26.5 2.8 %collective-permute-start.3 = (f32[15,64,128]{2,1,0:T(8,128)S(1)}, f32[15,64,128]{2,1,0:T(8,128)S(1)}, u32[]{:S(2)}, u32[]{:S(2)}) collective-permute-start(f32[15,64,128]{2,1,0:T(8,128)S(1)} %get-tuple-element.23), channel_id=1, source_target_pairs={{0,1},{1,0},{2,3},{3,2},{4,5},{5,4},{6,7},{7,6},{8,9},{9,8},{10,11... | collective-permute-start | bytes 1474568 | tf_op jit(solution)/shard_map/ppermute | solution.py:266
  29.4 2.3 %collective-permute-done.5.re = f32[9,64,128]{2,1,0:T(8,128)S(1)} collective-permute-done((f32[9,64,128]{2,1,0:T(8,128)S(1)}, f32[9,64,128]{2,1,0:T(8,128)S(1)}, u32[]{:S(2)}, u32[]{:S(2)}) %collective-permute-start.5) | collective-permute-done | bytes 294944 | tf_op jit(solution)/shard_map/ppermute | solution.py:266
  31.7 0.8 %shard_map.58 = (f32[9,128,128]{2,1,0:T(8,128)S(1)}, f32[9,64,128]{2,1,0:T(8,128)S(1)}, f32[9,64,128]{2,1,0:T(8,128)S(1)}) custom-call(bf16[256,384]{1,0:T(8,128)(2,1)S(1)} %copy-done.1, f32[24,128,128]{2,1,0:T(8,128)S(1)} %bitcast.4, f32[9,64,128]{2,1,0:T(8,128)S(1)} %collective-permute-done.4.ro, f32[9,64,128]{2,1,0:T(8,128)S(1)} %collective-permute-done.5.re), custom_call_target="tpu_custom_call" | custom-call | tf_op jit(solution)/shard_map/pallas_call | solution.py:249
  32.5 1.9 %collective-permute-start.6 = (f32[9,64,128]{2,1,0:T(8,128)S(1)}, f32[9,64,128]{2,1,0:T(8,128)S(1)}, u32[]{:S(2)}, u32[]{:S(2)}) collective-permute-start(f32[9,64,128]{2,1,0:T(8,128)S(1)} %get-tuple-element.27), channel_id=1, source_target_pairs={{32,64},{64,32},{96,128},{128,96},{160,192},{192,160},{224,256},{2... | collective-permute-start | bytes 884744 | tf_op jit(solution)/shard_map/ppermute | solution.py:266
  34.5 4.8 %collective-permute-start.7 = (f32[9,64,128]{2,1,0:T(8,128)S(1)}, f32[9,64,128]{2,1,0:T(8,128)S(1)}, u32[]{:S(2)}, u32[]{:S(2)}) collective-permute-start(f32[9,64,128]{2,1,0:T(8,128)S(1)} %get-tuple-element.28), channel_id=1, source_target_pairs={{0,32},{32,0},{64,96},{96,64},{128,160},{160,128},{192,224},{224,1... | collective-permute-start | bytes 884744 | tf_op jit(solution)/shard_map/ppermute | solution.py:266
  39.3 1.3 %collective-permute-done.6.refs_2_ = f32[9,64,128]{2,1,0:T(8,128)S(1)} collective-permute-done((f32[9,64,128]{2,1,0:T(8,128)S(1)}, f32[9,64,128]{2,1,0:T(8,128)S(1)}, u32[]{:S(2)}, u32[]{:S(2)}) %collective-permute-start.6) | collective-permute-done | bytes 294944 | tf_op jit(solution)/shard_map/ppermute | solution.py:266
  40.6 0.9 %shard_map.59 = (f32[9,128,128]{2,1,0:T(8,128)S(1)}, f32[128,128]{1,0:T(8,128)S(1)}) custom-call(bf16[384,256]{1,0:T(8,128)(2,1)S(1)} %copy-done.2, f32[9,128,128]{2,1,0:T(8,128)S(1)} %get-tuple-element.26.refs_1_, f32[9,64,128]{2,1,0:T(8,128)S(1)} %collective-permute-done.6.refs_2_, f32[9,64,128]{2,1,0:T(8,128)S(1)} %collective-permute-done.7.refs_3_), custom_call_target="tpu_custom_call" | custom-call | tf_op jit(solution)/shard_map/pallas_call | solution.py:249
  41.5 0.1 collective-permute-done.2.refs_2_
  41.6 1.5 %shard_map.60 = (f32[15,128,128]{2,1,0:T(8,128)S(1)}, f32[8,48,128]{2,1,0:T(8,128)S(1)}) custom-call(bf16[256,384]{1,0:T(8,128)(2,1)S(1)} %copy-done.1, f32[15,128,128]{2,1,0:T(8,128)S(1)} %get-tuple-element.21.refs_1_, f32[15,64,128]{2,1,0:T(8,128)S(1)} %collective-permute-done.2.refs_2_, f32[15,64,128]{2,1,0:T(8,128)S(1)} %collective-permute-done.3.refs_3_, ...), custom_call_target="tpu_custom_call" | custom-call | tf_op jit(solution)/shard_map/pallas_call | solution.py:249
  43.1 14.4 %all_to_all.10.st = f32[8,48,128]{2,1,0:T(8,128)S(1)} all-to-all(f32[8,48,128]{2,1,0:T(8,128)S(1)} %get-tuple-element.32), channel_id=1, replica_groups={{0,1,2,3,4,5,6,7},{8,9,10,11,12,13,14,15},{16,17,18,19,20,21,22,23},{24..., dimensions={0} | all-to-all | bytes 393216 | tf_op jit(solution)/shard_map/all_to_all | solution.py:310
  57.6 0.7 shard_map.61
  58.2 3.3 %all-to-all-start.1 = ((f32[4,48,128]{2,1,0:T(8,128)}), f32[4,48,128]{2,1,0:T(8,128)S(1)}, u32[]{:S(2)}, u32[]{:S(2)}) async-start(f32[4,48,128]{2,1,0:T(8,128)} %shard_map.61), calls=%async_computation.1 | async-start | bytes 196608 | tf_op jit(solution)/shard_map/all_to_all | solution.py:312
  61.6 0.4 shard_map.62.wide
  61.9 5.4 %all-to-all-done.1.st = f32[4,48,128]{2,1,0:T(8,128)S(1)} async-done(((f32[4,48,128]{2,1,0:T(8,128)}), f32[4,48,128]{2,1,0:T(8,128)S(1)}, u32[]{:S(2)}, u32[]{:S(2)}) %all-to-all-start.1) | async-done | bytes 98336 | tf_op jit(solution)/shard_map/all_to_all | solution.py:312
  67.3 1.8 %shard_map.63 = f32[8,3,128,128]{3,2,1,0:T(8,128)} custom-call(f32[15,128,128]{2,1,0:T(8,128)S(1)} %get-tuple-element.30.fb, f32[9,128,128]{2,1,0:T(8,128)S(1)} %get-tuple-element.31.fa, f32[4,48,128]{2,1,0:T(8,128)S(1)} %all-to-all-done.1.st, f32[7,128,128]{2,1,0:T(8,128)S(1)} %shard_map.62.wide), custom_call_target="tpu_custom_call" | custom-call | tf_op jit(solution)/shard_map/pallas_call | solution.py:249
  (14 shorter events, 0.0 us)
Async XLA Ops:
  0.0 6.9 %copy-start = (f32[8,3,128,128]{3,2,1,0:T(8,128)S(1)}, f32[8,3,128,128]{3,2,1,0:T(8,128)}, u32[]{:S(2)}) copy-start(f32[8,3,128,128]{3,2,1,0:T(8,128)} %param.5) | copy-start | bytes 4718596
  0.0 22.3 %copy-start.2 = (bf16[384,256]{1,0:T(8,128)(2,1)S(1)}, bf16[384,256]{1,0:T(8,128)(2,1)}, u32[]{:S(2)}) copy-start(bf16[384,256]{1,0:T(8,128)(2,1)} %constant.5.clone.bt.refs_0_) | copy-start | bytes 589828
  1.3 21.0 %collective-permute-start = (f32[15,64,128]{2,1,0:T(8,128)S(1)}, f32[15,64,128]{2,1,0:T(8,128)S(1)}, u32[]{:S(2)}, u32[]{:S(2)}) collective-permute-start(f32[15,64,128]{2,1,0:T(8,128)S(1)} %get-tuple-element.19), channel_id=1, source_target_pairs={{32,64},{64,32},{96,128},{128,96},{160,192},{192,160},{224,256},{2... | collective-permute-start | bytes 1474568 | tf_op jit(solution)/shard_map/ppermute | solution.py:266
  3.3 19.1 %collective-permute-start.1 = (f32[15,64,128]{2,1,0:T(8,128)S(1)}, f32[15,64,128]{2,1,0:T(8,128)S(1)}, u32[]{:S(2)}, u32[]{:S(2)}) collective-permute-start(f32[15,64,128]{2,1,0:T(8,128)S(1)} %get-tuple-element.20), channel_id=1, source_target_pairs={{0,32},{32,0},{64,96},{96,64},{128,160},{160,128},{192,224},{224,1... | collective-permute-start | bytes 1474568 | tf_op jit(solution)/shard_map/ppermute | solution.py:266
  7.1 24.6 %copy-start.1 = (bf16[256,384]{1,0:T(8,128)(2,1)S(1)}, bf16[256,384]{1,0:T(8,128)(2,1)}, u32[]{:S(2)}) copy-start(bf16[256,384]{1,0:T(8,128)(2,1)} %constant.4.clone.b.refs_0_) | copy-start | bytes 589828
  7.1 22.3 %collective-permute-start.4 = (f32[9,64,128]{2,1,0:T(8,128)S(1)}, f32[9,64,128]{2,1,0:T(8,128)S(1)}, u32[]{:S(2)}, u32[]{:S(2)}) collective-permute-start(f32[9,64,128]{2,1,0:T(8,128)S(1)} %get-tuple-element.24), channel_id=1, source_target_pairs={{1,2},{2,1},{3,4},{4,3},{5,6},{6,5},{7,8},{8,7},{9,10},{10,9},{11,... | collective-permute-start | bytes 884744 | tf_op jit(solution)/shard_map/ppermute | solution.py:266
  20.4 11.3 %collective-permute-start.5 = (f32[9,64,128]{2,1,0:T(8,128)S(1)}, f32[9,64,128]{2,1,0:T(8,128)S(1)}, u32[]{:S(2)}, u32[]{:S(2)}) collective-permute-start(f32[9,64,128]{2,1,0:T(8,128)S(1)} %get-tuple-element.25), channel_id=1, source_target_pairs={{0,1},{1,0},{2,3},{3,2},{4,5},{5,4},{6,7},{7,6},{8,9},{9,8},{10,11... | collective-permute-start | bytes 884744 | tf_op jit(solution)/shard_map/ppermute | solution.py:266
  23.5 18.1 %collective-permute-start.2 = (f32[15,64,128]{2,1,0:T(8,128)S(1)}, f32[15,64,128]{2,1,0:T(8,128)S(1)}, u32[]{:S(2)}, u32[]{:S(2)}) collective-permute-start(f32[15,64,128]{2,1,0:T(8,128)S(1)} %get-tuple-element.22), channel_id=1, source_target_pairs={{1,2},{2,1},{3,4},{4,3},{5,6},{6,5},{7,8},{8,7},{9,10},{10,9},{11,... | collective-permute-start | bytes 1474568 | tf_op jit(solution)/shard_map/ppermute | solution.py:266
  26.5 15.1 %collective-permute-start.3 = (f32[15,64,128]{2,1,0:T(8,128)S(1)}, f32[15,64,128]{2,1,0:T(8,128)S(1)}, u32[]{:S(2)}, u32[]{:S(2)}) collective-permute-start(f32[15,64,128]{2,1,0:T(8,128)S(1)} %get-tuple-element.23), channel_id=1, source_target_pairs={{0,1},{1,0},{2,3},{3,2},{4,5},{5,4},{6,7},{7,6},{8,9},{9,8},{10,11... | collective-permute-start | bytes 1474568 | tf_op jit(solution)/shard_map/ppermute | solution.py:266
  32.5 8.0 %collective-permute-start.6 = (f32[9,64,128]{2,1,0:T(8,128)S(1)}, f32[9,64,128]{2,1,0:T(8,128)S(1)}, u32[]{:S(2)}, u32[]{:S(2)}) collective-permute-start(f32[9,64,128]{2,1,0:T(8,128)S(1)} %get-tuple-element.27), channel_id=1, source_target_pairs={{32,64},{64,32},{96,128},{128,96},{160,192},{192,160},{224,256},{2... | collective-permute-start | bytes 884744 | tf_op jit(solution)/shard_map/ppermute | solution.py:266
  34.5 6.1 %collective-permute-start.7 = (f32[9,64,128]{2,1,0:T(8,128)S(1)}, f32[9,64,128]{2,1,0:T(8,128)S(1)}, u32[]{:S(2)}, u32[]{:S(2)}) collective-permute-start(f32[9,64,128]{2,1,0:T(8,128)S(1)} %get-tuple-element.28), channel_id=1, source_target_pairs={{0,32},{32,0},{64,96},{96,64},{128,160},{160,128},{192,224},{224,1... | collective-permute-start | bytes 884744 | tf_op jit(solution)/shard_map/ppermute | solution.py:266
  41.5 20.1 %copy-start.3 = (f32[6,128]{1,0:T(8,128)S(1)}, f32[6,128]{1,0:T(8,128)}, u32[]{:S(2)}) copy-start(f32[6,128]{1,0:T(8,128)} %stress.1) | copy-start | bytes 9220
  41.5 20.1 %copy-start.4 = (f32[128]{0:T(128)S(1)}, f32[128]{0:T(128)}, u32[]{:S(2)}) copy-start(f32[128]{0:T(128)} %profile.1) | copy-start | bytes 1540
  58.2 9.1 %all-to-all-start.1 = ((f32[4,48,128]{2,1,0:T(8,128)}), f32[4,48,128]{2,1,0:T(8,128)S(1)}, u32[]{:S(2)}, u32[]{:S(2)}) async-start(f32[4,48,128]{2,1,0:T(8,128)} %shard_map.61), calls=%async_computation.1 | async-start | bytes 196608 | tf_op jit(solution)/shard_map/all_to_all | solution.py:312

commit v5 on v4

--- a/solution.py
+++ b/solution.py
@@ -110,23 +110,21 @@
     return [range(i, min(i + step, n)) for i in range(0, n, step)]
 
 
-def pack_y_kernel(src, yo, ye, sems):
+def pack_y_kernel(src, yo, sem):
     off = pl.multiple_of(parity("wn") * H, H)
-    opp = pl.multiple_of(H - off, H)
-    one = pltpu.make_async_copy(src.at[pl.ds(0, NB), pl.ds(off, H)], yo, sems.at[0])
-    two = pltpu.make_async_copy(src.at[pl.ds(0, NB), pl.ds(opp, H)], ye, sems.at[1])
-    one.start()
-    two.start()
-    one.wait()
-    two.wait()
-
-
-def pack_z_kernel(x, zo, ze):
-    zeven = parity("sp") == 0
+    copy = pltpu.make_async_copy(src.at[pl.ds(0, NB), pl.ds(off, H)], yo, sem.at[0])
+    copy.start()
+    copy.wait()
+
+
+def pack_z_kernel(x, zo, ze, ye):
+    zeven, yeven = parity("sp") == 0, parity("wn") == 0
     for p in range(NA):
         e, o = edges(x[NB + p], zeven)
         ze[p] = e
         zo[p] = o
+    for p in range(NB):
+        ye[p] = jnp.where(yeven, x[p, H:], x[p, :H])
 
 
 def y_first_kernel(bt, x, ro, re, n, zo, ze):
@@ -277,15 +275,11 @@
     b, bt = (jnp.asarray(v) for v in bands())
     hb, ha = (NB, H, T), (NA, H, T)
     fb, fa = (NB, T, T), (NA, T, T)
-    yo, ye = call(
-        pack_y_kernel,
-        [x],
-        [hb, hb],
-        scratch=[pltpu.SemaphoreType.DMA((2,))],
-        hbm_in=(0,),
+    (yo,) = call(
+        pack_y_kernel, [x], [hb], scratch=[pltpu.SemaphoreType.DMA((1,))], hbm_in=(0,)
     )
     yo = swap(yo, "wn", 1, False)
-    zo, ze = call(pack_z_kernel, [x], [ha, ha])
+    zo, ze, ye = call(pack_z_kernel, [x], [ha, ha, hb])
     zo = swap(zo, "sp", 1, True)
     ye = swap(ye, "wn", 0, False)
     ze = swap(ze, "sp", 0, True)

time: 69.6 us -> 72.1 us (1.036)
  the two profiles are of different devices: /device:TPU:16 before, /device:TPU:24 now
where the time goes in v5:
time: 72.1 us; the launch traced here: 71.6 us
  starting transfers between devices  38.6 us (54%)
  blocking collectives  13.9 us (19%)
  waiting for transfers between devices  8.93 us (12%)
  Pallas kernels  8.58 us (12%)
  local copies, waits for them, and re-layouts  1.43 us (2%)
    ppermute x8, starting transfers between devices, swap(): return lax.ppermute(v, axis, pairs)  35.3 us
    all_to_all x1, blocking collectives, run(): st = lax.all_to_all(st, 'sp', 0, 0, axis_index_groups=zs, tiled=True)  13.9 us
    pallas_call x9, Pallas kernels, call(): pl.pallas_call(kernel, in_specs=specs, out_specs=out_specs, out_shape=sha...  8.58 us
    all_to_all x1, waiting for transfers between devices, run(): st = lax.all_to_all(st, 'sp', 0, 0, axis_index_groups=xs, tiled=True)  5.39 us
    ppermute x8, waiting for transfers between devices, swap(): return lax.ppermute(v, axis, pairs)  3.54 us
    all_to_all x1, starting transfers between devices, run(): st = lax.all_to_all(st, 'sp', 0, 0, axis_index_groups=xs, tiled=True)  3.3 us
  transfers between devices with their start and end apart: 9, of which 4 were waited for; matrix products, arithmetic and copies ran while one was open for 0% of the time, Pallas kernels for 6%

profile of v5, /device:TPU:24, one launch (start us, length us, event | category | flops | bytes accessed | tf_op | source)
XLA Modules:
  0.0 71.6 jit_solution(9345596439346160827)
XLA Ops:
  0.0 1.4 %copy-done = f32[8,3,128,128]{3,2,1,0:T(8,128)S(1)} copy-done((f32[8,3,128,128]{3,2,1,0:T(8,128)S(1)}, f32[8,3,128,128]{3,2,1,0:T(8,128)}, u32[]{:S(2)}) %copy-start) | copy-done | bytes 1572888
  1.4 0.2 shard_map.56
  1.7 2.1 %collective-permute-start.1 = (f32[15,64,128]{2,1,0:T(8,128)S(1)}, f32[15,64,128]{2,1,0:T(8,128)S(1)}, u32[]{:S(2)}, u32[]{:S(2)}) collective-permute-start(f32[15,64,128]{2,1,0:T(8,128)S(1)} %get-tuple-element.18), channel_id=1, source_target_pairs={{0,32},{32,0},{64,96},{96,64},{128,160},{160,128},{192,224},{224,1... | collective-permute-start | bytes 1474568 | tf_op jit(solution)/shard_map/ppermute | solution.py:264
  3.7 1.1 %shard_map.55 = f32[15,64,128]{2,1,0:T(8,128)S(1)} custom-call(f32[24,128,128]{2,1,0:T(8,128)} %bitcast.1), custom_call_target="tpu_custom_call" | custom-call | tf_op jit(solution)/shard_map/pallas_call | solution.py:247
  4.8 2.6 %collective-permute-start = (f32[15,64,128]{2,1,0:T(8,128)S(1)}, f32[15,64,128]{2,1,0:T(8,128)S(1)}, u32[]{:S(2)}, u32[]{:S(2)}) collective-permute-start(f32[15,64,128]{2,1,0:T(8,128)S(1)} %shard_map.55), channel_id=1, source_target_pairs={{32,64},{64,32},{96,128},{128,96},{160,192},{192,160},{224,256},{2... | collective-permute-start | bytes 1474568 | tf_op jit(solution)/shard_map/ppermute | solution.py:264
  7.4 13.1 %collective-permute-start.4 = (f32[9,64,128]{2,1,0:T(8,128)S(1)}, f32[9,64,128]{2,1,0:T(8,128)S(1)}, u32[]{:S(2)}, u32[]{:S(2)}) collective-permute-start(f32[9,64,128]{2,1,0:T(8,128)S(1)} %get-tuple-element.22), channel_id=1, source_target_pairs={{1,2},{2,1},{3,4},{4,3},{5,6},{6,5},{7,8},{8,7},{9,10},{10,9},{11,... | collective-permute-start | bytes 884744 | tf_op jit(solution)/shard_map/ppermute | solution.py:264
  20.5 1.9 %collective-permute-start.5 = (f32[9,64,128]{2,1,0:T(8,128)S(1)}, f32[9,64,128]{2,1,0:T(8,128)S(1)}, u32[]{:S(2)}, u32[]{:S(2)}) collective-permute-start(f32[9,64,128]{2,1,0:T(8,128)S(1)} %get-tuple-element.23), channel_id=1, source_target_pairs={{0,1},{1,0},{2,3},{3,2},{4,5},{5,4},{6,7},{7,6},{8,9},{9,8},{10,11... | collective-permute-start | bytes 884744 | tf_op jit(solution)/shard_map/ppermute | solution.py:264
  22.5 1.1 %shard_map.57 = (f32[15,128,128]{2,1,0:T(8,128)S(1)}, f32[15,64,128]{2,1,0:T(8,128)S(1)}, f32[15,64,128]{2,1,0:T(8,128)S(1)}) custom-call(bf16[384,256]{1,0:T(8,128)(2,1)S(1)} %copy-done.3, f32[24,128,128]{2,1,0:T(8,128)S(1)} %bitcast.3, f32[15,64,128]{2,1,0:T(8,128)S(1)} %collective-permute-done.ro, f32[15,64,128]{2,1,0:T(8,128)S(1)} %collective-permute-done.1.re), custom_call_target="tpu_custom_call" | custom-call | tf_op jit(solution)/shard_map/pallas_call | solution.py:247
  23.7 5.7 %collective-permute-start.2 = (f32[15,64,128]{2,1,0:T(8,128)S(1)}, f32[15,64,128]{2,1,0:T(8,128)S(1)}, u32[]{:S(2)}, u32[]{:S(2)}) collective-permute-start(f32[15,64,128]{2,1,0:T(8,128)S(1)} %get-tuple-element.20), channel_id=1, source_target_pairs={{1,2},{2,1},{3,4},{4,3},{5,6},{6,5},{7,8},{8,7},{9,10},{10,9},{11,... | collective-permute-start | bytes 1474568 | tf_op jit(solution)/shard_map/ppermute | solution.py:264
  29.4 1.9 %collective-permute-start.3 = (f32[15,64,128]{2,1,0:T(8,128)S(1)}, f32[15,64,128]{2,1,0:T(8,128)S(1)}, u32[]{:S(2)}, u32[]{:S(2)}) collective-permute-start(f32[15,64,128]{2,1,0:T(8,128)S(1)} %get-tuple-element.21), channel_id=1, source_target_pairs={{0,1},{1,0},{2,3},{3,2},{4,5},{5,4},{6,7},{7,6},{8,9},{9,8},{10,11... | collective-permute-start | bytes 1474568 | tf_op jit(solution)/shard_map/ppermute | solution.py:264
  31.3 0.8 %shard_map.58 = (f32[9,128,128]{2,1,0:T(8,128)S(1)}, f32[9,64,128]{2,1,0:T(8,128)S(1)}, f32[9,64,128]{2,1,0:T(8,128)S(1)}) custom-call(bf16[256,384]{1,0:T(8,128)(2,1)S(1)} %copy-done.2, f32[24,128,128]{2,1,0:T(8,128)S(1)} %bitcast.4, f32[9,64,128]{2,1,0:T(8,128)S(1)} %collective-permute-done.4.ro, f32[9,64,128]{2,1,0:T(8,128)S(1)} %collective-permute-done.5.re), custom_call_target="tpu_custom_call" | custom-call | tf_op jit(solution)/shard_map/pallas_call | solution.py:247
  32.2 2.8 %collective-permute-start.6 = (f32[9,64,128]{2,1,0:T(8,128)S(1)}, f32[9,64,128]{2,1,0:T(8,128)S(1)}, u32[]{:S(2)}, u32[]{:S(2)}) collective-permute-start(f32[9,64,128]{2,1,0:T(8,128)S(1)} %get-tuple-element.25), channel_id=1, source_target_pairs={{32,64},{64,32},{96,128},{128,96},{160,192},{192,160},{224,256},{2... | collective-permute-start | bytes 884744 | tf_op jit(solution)/shard_map/ppermute | solution.py:264
  35.0 5.1 %collective-permute-start.7 = (f32[9,64,128]{2,1,0:T(8,128)S(1)}, f32[9,64,128]{2,1,0:T(8,128)S(1)}, u32[]{:S(2)}, u32[]{:S(2)}) collective-permute-start(f32[9,64,128]{2,1,0:T(8,128)S(1)} %get-tuple-element.26), channel_id=1, source_target_pairs={{0,32},{32,0},{64,96},{96,64},{128,160},{160,128},{192,224},{224,1... | collective-permute-start | bytes 884744 | tf_op jit(solution)/shard_map/ppermute | solution.py:264
  40.1 0.1 collective-permute-done.6.refs_2_
  40.2 1.1 %collective-permute-done.7.refs_3_ = f32[9,64,128]{2,1,0:T(8,128)S(1)} collective-permute-done((f32[9,64,128]{2,1,0:T(8,128)S(1)}, f32[9,64,128]{2,1,0:T(8,128)S(1)}, u32[]{:S(2)}, u32[]{:S(2)}) %collective-permute-start.7) | collective-permute-done | bytes 294944 | tf_op jit(solution)/shard_map/ppermute | solution.py:264
  41.3 0.9 %shard_map.59 = (f32[9,128,128]{2,1,0:T(8,128)S(1)}, f32[128,128]{1,0:T(8,128)S(1)}) custom-call(bf16[384,256]{1,0:T(8,128)(2,1)S(1)} %copy-done.3, f32[9,128,128]{2,1,0:T(8,128)S(1)} %get-tuple-element.24.refs_1_, f32[9,64,128]{2,1,0:T(8,128)S(1)} %collective-permute-done.6.refs_2_, f32[9,64,128]{2,1,0:T(8,128)S(1)} %collective-permute-done.7.refs_3_), custom_call_target="tpu_custom_call" | custom-call | tf_op jit(solution)/shard_map/pallas_call | solution.py:247
  42.3 2.3 %collective-permute-done.3.refs_3_ = f32[15,64,128]{2,1,0:T(8,128)S(1)} collective-permute-done((f32[15,64,128]{2,1,0:T(8,128)S(1)}, f32[15,64,128]{2,1,0:T(8,128)S(1)}, u32[]{:S(2)}, u32[]{:S(2)}) %collective-permute-start.3) | collective-permute-done | bytes 491552 | tf_op jit(solution)/shard_map/ppermute | solution.py:264
  44.6 1.5 %shard_map.60 = (f32[15,128,128]{2,1,0:T(8,128)S(1)}, f32[8,48,128]{2,1,0:T(8,128)S(1)}) custom-call(bf16[256,384]{1,0:T(8,128)(2,1)S(1)} %copy-done.2, f32[15,128,128]{2,1,0:T(8,128)S(1)} %get-tuple-element.19.refs_1_, f32[15,64,128]{2,1,0:T(8,128)S(1)} %collective-permute-done.2.refs_2_, f32[15,64,128]{2,1,0:T(8,128)S(1)} %collective-permute-done.3.refs_3_, ...), custom_call_target="tpu_custom_call" | custom-call | tf_op jit(solution)/shard_map/pallas_call | solution.py:247
  46.2 13.9 %all_to_all.10.st = f32[8,48,128]{2,1,0:T(8,128)S(1)} all-to-all(f32[8,48,128]{2,1,0:T(8,128)S(1)} %get-tuple-element.30), channel_id=1, replica_groups={{0,1,2,3,4,5,6,7},{8,9,10,11,12,13,14,15},{16,17,18,19,20,21,22,23},{24..., dimensions={0} | all-to-all | bytes 393216 | tf_op jit(solution)/shard_map/all_to_all | solution.py:304
  60.0 0.7 shard_map.61
  60.7 3.3 %all-to-all-start.1 = ((f32[4,48,128]{2,1,0:T(8,128)}), f32[4,48,128]{2,1,0:T(8,128)S(1)}, u32[]{:S(2)}, u32[]{:S(2)}) async-start(f32[4,48,128]{2,1,0:T(8,128)} %shard_map.61), calls=%async_computation.1 | async-start | bytes 196608 | tf_op jit(solution)/shard_map/all_to_all | solution.py:306
  64.0 0.4 shard_map.62.wide
  64.4 5.4 %all-to-all-done.1.st = f32[4,48,128]{2,1,0:T(8,128)S(1)} async-done(((f32[4,48,128]{2,1,0:T(8,128)}), f32[4,48,128]{2,1,0:T(8,128)S(1)}, u32[]{:S(2)}, u32[]{:S(2)}) %all-to-all-start.1) | async-done | bytes 98336 | tf_op jit(solution)/shard_map/all_to_all | solution.py:306
  69.8 1.8 %shard_map.63 = f32[8,3,128,128]{3,2,1,0:T(8,128)} custom-call(f32[15,128,128]{2,1,0:T(8,128)S(1)} %get-tuple-element.28.fb, f32[9,128,128]{2,1,0:T(8,128)S(1)} %get-tuple-element.29.fa, f32[4,48,128]{2,1,0:T(8,128)S(1)} %all-to-all-done.1.st, f32[7,128,128]{2,1,0:T(8,128)S(1)} %shard_map.62.wide), custom_call_target="tpu_custom_call" | custom-call | tf_op jit(solution)/shard_map/pallas_call | solution.py:247
  (16 shorter events, 0.0 us)
Async XLA Ops:
  0.0 1.4 %copy-start = (f32[8,3,128,128]{3,2,1,0:T(8,128)S(1)}, f32[8,3,128,128]{3,2,1,0:T(8,128)}, u32[]{:S(2)}) copy-start(f32[8,3,128,128]{3,2,1,0:T(8,128)} %param.5) | copy-start | bytes 4718596
  1.4 21.1 %copy-start.1 = (f32[8,3,128,128]{3,2,1,0:T(8,128)S(1)}, f32[8,3,128,128]{3,2,1,0:T(8,128)}, u32[]{:S(2)}) copy-start(f32[8,3,128,128]{3,2,1,0:T(8,128)} %param.5) | copy-start | bytes 4718596
  1.4 21.1 %copy-start.3 = (bf16[384,256]{1,0:T(8,128)(2,1)S(1)}, bf16[384,256]{1,0:T(8,128)(2,1)}, u32[]{:S(2)}) copy-start(bf16[384,256]{1,0:T(8,128)(2,1)} %constant.5.clone.bt.refs_0_) | copy-start | bytes 589828
  1.7 20.8 %collective-permute-start.1 = (f32[15,64,128]{2,1,0:T(8,128)S(1)}, f32[15,64,128]{2,1,0:T(8,128)S(1)}, u32[]{:S(2)}, u32[]{:S(2)}) collective-permute-start(f32[15,64,128]{2,1,0:T(8,128)S(1)} %get-tuple-element.18), channel_id=1, source_target_pairs={{0,32},{32,0},{64,96},{96,64},{128,160},{160,128},{192,224},{224,1... | collective-permute-start | bytes 1474568 | tf_op jit(solution)/shard_map/ppermute | solution.py:264
  4.8 26.6 %copy-start.2 = (bf16[256,384]{1,0:T(8,128)(2,1)S(1)}, bf16[256,384]{1,0:T(8,128)(2,1)}, u32[]{:S(2)}) copy-start(bf16[256,384]{1,0:T(8,128)(2,1)} %constant.4.clone.b.refs_0_) | copy-start | bytes 589828
  4.8 17.7 %collective-permute-start = (f32[15,64,128]{2,1,0:T(8,128)S(1)}, f32[15,64,128]{2,1,0:T(8,128)S(1)}, u32[]{:S(2)}, u32[]{:S(2)}) collective-permute-start(f32[15,64,128]{2,1,0:T(8,128)S(1)} %shard_map.55), channel_id=1, source_target_pairs={{32,64},{64,32},{96,128},{128,96},{160,192},{192,160},{224,256},{2... | collective-permute-start | bytes 1474568 | tf_op jit(solution)/shard_map/ppermute | solution.py:264
  7.4 23.9 %collective-permute-start.4 = (f32[9,64,128]{2,1,0:T(8,128)S(1)}, f32[9,64,128]{2,1,0:T(8,128)S(1)}, u32[]{:S(2)}, u32[]{:S(2)}) collective-permute-start(f32[9,64,128]{2,1,0:T(8,128)S(1)} %get-tuple-element.22), channel_id=1, source_target_pairs={{1,2},{2,1},{3,4},{4,3},{5,6},{6,5},{7,8},{8,7},{9,10},{10,9},{11,... | collective-permute-start | bytes 884744 | tf_op jit(solution)/shard_map/ppermute | solution.py:264
  20.5 10.8 %collective-permute-start.5 = (f32[9,64,128]{2,1,0:T(8,128)S(1)}, f32[9,64,128]{2,1,0:T(8,128)S(1)}, u32[]{:S(2)}, u32[]{:S(2)}) collective-permute-start(f32[9,64,128]{2,1,0:T(8,128)S(1)} %get-tuple-element.23), channel_id=1, source_target_pairs={{0,1},{1,0},{2,3},{3,2},{4,5},{5,4},{6,7},{7,6},{8,9},{9,8},{10,11... | collective-permute-start | bytes 884744 | tf_op jit(solution)/shard_map/ppermute | solution.py:264
  23.7 18.6 %collective-permute-start.2 = (f32[15,64,128]{2,1,0:T(8,128)S(1)}, f32[15,64,128]{2,1,0:T(8,128)S(1)}, u32[]{:S(2)}, u32[]{:S(2)}) collective-permute-start(f32[15,64,128]{2,1,0:T(8,128)S(1)} %get-tuple-element.20), channel_id=1, source_target_pairs={{1,2},{2,1},{3,4},{4,3},{5,6},{6,5},{7,8},{8,7},{9,10},{10,9},{11,... | collective-permute-start | bytes 1474568 | tf_op jit(solution)/shard_map/ppermute | solution.py:264
  29.4 15.2 %collective-permute-start.3 = (f32[15,64,128]{2,1,0:T(8,128)S(1)}, f32[15,64,128]{2,1,0:T(8,128)S(1)}, u32[]{:S(2)}, u32[]{:S(2)}) collective-permute-start(f32[15,64,128]{2,1,0:T(8,128)S(1)} %get-tuple-element.21), channel_id=1, source_target_pairs={{0,1},{1,0},{2,3},{3,2},{4,5},{5,4},{6,7},{7,6},{8,9},{9,8},{10,11... | collective-permute-start | bytes 1474568 | tf_op jit(solution)/shard_map/ppermute | solution.py:264
  32.2 8.0 %collective-permute-start.6 = (f32[9,64,128]{2,1,0:T(8,128)S(1)}, f32[9,64,128]{2,1,0:T(8,128)S(1)}, u32[]{:S(2)}, u32[]{:S(2)}) collective-permute-start(f32[9,64,128]{2,1,0:T(8,128)S(1)} %get-tuple-element.25), channel_id=1, source_target_pairs={{32,64},{64,32},{96,128},{128,96},{160,192},{192,160},{224,256},{2... | collective-permute-start | bytes 884744 | tf_op jit(solution)/shard_map/ppermute | solution.py:264
  35.0 6.3 %collective-permute-start.7 = (f32[9,64,128]{2,1,0:T(8,128)S(1)}, f32[9,64,128]{2,1,0:T(8,128)S(1)}, u32[]{:S(2)}, u32[]{:S(2)}) collective-permute-start(f32[9,64,128]{2,1,0:T(8,128)S(1)} %get-tuple-element.26), channel_id=1, source_target_pairs={{0,32},{32,0},{64,96},{96,64},{128,160},{160,128},{192,224},{224,1... | collective-permute-start | bytes 884744 | tf_op jit(solution)/shard_map/ppermute | solution.py:264
  42.2 21.8 %copy-start.4 = (f32[6,128]{1,0:T(8,128)S(1)}, f32[6,128]{1,0:T(8,128)}, u32[]{:S(2)}) copy-start(f32[6,128]{1,0:T(8,128)} %stress.1) | copy-start | bytes 9220
  42.2 21.8 %copy-start.5 = (f32[128]{0:T(128)S(1)}, f32[128]{0:T(128)}, u32[]{:S(2)}) copy-start(f32[128]{0:T(128)} %profile.1) | copy-start | bytes 1540
  60.7 9.1 %all-to-all-start.1 = ((f32[4,48,128]{2,1,0:T(8,128)}), f32[4,48,128]{2,1,0:T(8,128)S(1)}, u32[]{:S(2)}, u32[]{:S(2)}) async-start(f32[4,48,128]{2,1,0:T(8,128)} %shard_map.61), calls=%async_computation.1 | async-start | bytes 196608 | tf_op jit(solution)/shard_map/all_to_all | solution.py:306
